TPU v7x, 32 devices: a whole 2x2x4 slice. The times are simulated.
32 devices in a mesh: ka: 8 (over y, x, core), slab: 4 (over z).
Axes of the slice: x: 2, y: 2, z: 4, core: 2. Of those that a mesh axis runs over, the one named last changes fastest.
Arguments:
- val_wave: float32 [2, 8, 2, 12, 16, 128], P(None, 'ka', None, 'slab'), may hold values from -6 to 6
- cond_wave: float32 [2, 8, 8, 12, 16, 128], P(None, 'ka', None, 'slab'), may hold values from -6 to 6
- val_energy: float32 [8, 2], P('ka'), may hold values from -2 to -0.5
- cond_energy: float32 [8, 8], P('ka'), may hold values from 0.5 to 3
- frequency: float32 [4], replicated, may hold values from 0.2 to 4
- kpoint_map: int32 [8], replicated, may hold values from 0 to 7, as said below
- umklapp: int32 [3, 8], replicated, may hold values from 0 to 1, as said below
- gvector_index: int32 [6144], replicated, may hold values from 0 to 24575, as said below
Outputs:
- polarizability: float32 [4, 2, 6144, 6144], P(None, None, 'ka', 'slab')
Inputs may be any that keep to these rules, and one draw needn't show every extreme that they name: With s the integer for which s * s * s = 8 and k = s * s * i + s * j + l, kpoint_map[k] is the index of (i + q0, j + q1, l + q2) taken modulo s in each coordinate, for one vector q whose components lie in 0 to s - 1, not all zero. umklapp[d, k] is 1 where coordinate d of k plus component d of q reaches s, else 0. `gvector_index`: entries are distinct.
All inputs are finite; a program needn't handle non-finite values.
Results may differ from a plain program's by a relative error of at most 0.0038.
Values may be sent and summed in bfloat16 or wider, within the bound.
A program may use at most 128 MiB of HBM per device.

v0:
```python
import math

import jax
import jax.numpy as jnp
from jax import lax
from jax.sharding import PartitionSpec as P

two_pi = 2.0 * math.pi
highest = lax.Precision.HIGHEST


def passed_along(block, axis, distance):
    devices = range(lax.axis_size(axis))
    route = [((i - distance) % len(devices), i) for i in devices]
    return lax.ppermute(block, axis, route)


def dft_table(length):
    index = jnp.arange(length, dtype=jnp.int32)
    angle = two_pi * (index[:, None] * index[None, :] % length).astype(jnp.float32) / length
    return (jnp.cos(angle), jnp.sin(angle))


def move_payload(payload, offset):
    return passed_along(payload, "ka", offset)


def route_grid(payload, heading, shift_coord, own_coord, grid_side):
    for grid_dim in range(3):
        stride = grid_side ** (2 - grid_dim)
        for bit_pos in range(grid_side.bit_length() - 1):
            hop_size = 1 << bit_pos
            direct = move_payload(payload, -heading * hop_size * stride)
            beside_all = move_payload(payload, -heading * (hop_size - grid_side) * stride)
            target = own_coord[grid_dim] + heading * hop_size
            inside = (target >= 0) & (target < grid_side)
            chosen = shift_coord[grid_dim] // hop_size % 2 == 1
            payload = jax.tree.map(
                lambda direct_one, around_one, staying: jnp.where(
                    chosen, jnp.where(inside, direct_one, around_one), staying
                ),
                direct,
                beside_all,
                payload,
            )
    return payload


def per_device(
    val_wave, cond_wave, val_energy, cond_energy, frequency, kpoint_map, umklapp, gvector_index
):
    slab_count = lax.axis_size("slab")
    kpoint_count = lax.axis_size("ka")
    kpoint_here = lax.axis_index("ka")
    slab_here = lax.axis_index("slab")
    grid_side = max((candidate for candidate in range(1, 9) if candidate**3 <= kpoint_count))
    shift_flat = kpoint_map[0]
    shift_coord = [shift_flat // grid_side ** (2 - grid_dim) % grid_side for grid_dim in range(3)]
    own_coord = [kpoint_here // grid_side ** (2 - grid_dim) % grid_side for grid_dim in range(3)]
    cond_wave, cond_energy = route_grid(
        (cond_wave, cond_energy), 1, shift_coord, own_coord, grid_side
    )
    shift_vec = jnp.sum(
        jnp.where(jnp.arange(kpoint_count, dtype=jnp.int32)[None, :] == kpoint_here, umklapp, 0),
        axis=1,
    )
    valence = val_wave[:, 0]
    conduct = cond_wave[:, 0]
    planes = valence.shape[2]
    extent_y = valence.shape[3]
    extent_z = valence.shape[4]
    extent_x = planes * slab_count
    xpos = slab_here * planes + jnp.arange(planes, dtype=jnp.int32)
    ypos = jnp.arange(extent_y, dtype=jnp.int32)
    zpos = jnp.arange(extent_z, dtype=jnp.int32)
    first_part = (shift_vec[0] * xpos % extent_x).astype(jnp.float32)[:, None, None] / extent_x
    second_part = (shift_vec[1] * ypos % extent_y).astype(jnp.float32)[None, :, None] / extent_y
    third_part = (shift_vec[2] * zpos % extent_z).astype(jnp.float32)[None, None, :] / extent_z
    angle = two_pi * (first_part + second_part + third_part)
    cosine = jnp.cos(angle)
    sine = jnp.sin(angle)
    cond_re = conduct[0] * cosine - conduct[1] * sine
    cond_im = conduct[0] * sine + conduct[1] * cosine
    dens_re = valence[0][:, None] * cond_re[None] + valence[1][:, None] * cond_im[None]
    dens_im = valence[0][:, None] * cond_im[None] - valence[1][:, None] * cond_re[None]
    pairs = dens_re.shape[0] * dens_re.shape[1]
    field = jnp.concatenate([dens_re, dens_im], axis=-1).reshape(
        pairs, planes, extent_y, 2 * extent_z
    )
    zcos, zsin = dft_table(extent_z)
    ztable = jnp.concatenate(
        [jnp.concatenate([zcos, -zsin], 1), jnp.concatenate([zsin, zcos], 1)], 0
    )
    field = jnp.dot(field, ztable, precision=highest, preferred_element_type=jnp.float32)
    ycos, ysin = dft_table(extent_y)
    swapped = jnp.concatenate([field[..., extent_z:], -field[..., :extent_z]], -1)
    field = jnp.einsum("ky,pxyz->pxkz", ycos, field, precision=highest) + jnp.einsum(
        "ky,pxyz->pxkz", ysin, swapped, precision=highest
    )
    flat = field.reshape(pairs, planes, extent_y * 2 * extent_z)
    gx_idx = gvector_index // (extent_y * extent_z)
    gy_idx = gvector_index // extent_z % extent_y
    gz_idx = gvector_index % extent_z
    column = gy_idx * (2 * extent_z) + gz_idx
    part_re = jnp.take(flat, column, axis=2)
    part_im = jnp.take(flat, column + extent_z, axis=2)
    xangle = two_pi * (xpos[:, None] * gx_idx[None, :] % extent_x).astype(jnp.float32) / extent_x
    xcos = jnp.cos(xangle)
    xsin = jnp.sin(xangle)
    norm = 1.0 / (2.0 * math.sqrt(extent_x * extent_y * extent_z))
    pair_re = jnp.sum(part_re * xcos + part_im * xsin, axis=1) * norm
    pair_im = jnp.sum(part_im * xcos - part_re * xsin, axis=1) * norm
    partial_value = jnp.stack([pair_re, pair_im])
    gap = (val_energy[0][:, None] - cond_energy[0][None, :]).reshape(pairs)
    weight = 2.0 * gap[None, :] / (gap[None, :] ** 2 + frequency[:, None] ** 2) / kpoint_count
    freq_count = frequency.shape[0]
    total_g = gvector_index.shape[0]
    block_g = total_g // slab_count
    row_g = total_g // kpoint_count
    whole = lax.psum(partial_value, "slab")
    block = lax.dynamic_slice_in_dim(whole, slab_here * block_g, block_g, 2)
    column_side = block.astype(jnp.bfloat16)
    rows_all = (whole[:, :, None, :] * jnp.transpose(weight)[None, :, :, None]).astype(
        jnp.bfloat16
    )[:, None]
    routed = lax.all_to_all(rows_all, "ka", split_axis=4, concat_axis=1, tiled=True)
    columns = lax.all_gather(column_side[:, None], "ka", axis=1, tiled=True)
    flat_rows = kpoint_count * pairs
    real_rows = routed[0].reshape(flat_rows, freq_count, row_g)
    imag_rows = routed[1].reshape(flat_rows, freq_count, row_g)
    left = jnp.stack(
        [jnp.concatenate([real_rows, imag_rows], 0), jnp.concatenate([imag_rows, -real_rows], 0)],
        axis=2,
    )
    left = left.reshape(2 * flat_rows, freq_count * 2 * row_g)
    right = columns.reshape(2 * flat_rows, block_g)
    product = lax.dot_general(
        left, right, (((0,), (0,)), ((), ())), preferred_element_type=jnp.float32
    )
    return product.reshape(freq_count, 2, row_g, block_g)


def solution(mesh):
    return jax.shard_map(
        per_device,
        mesh=mesh,
        in_specs=(
            P(None, "ka", None, "slab", None, None),
            P(None, "ka", None, "slab", None, None),
            P("ka", None),
            P("ka", None),
            P(),
            P(),
            P(),
            P(),
        ),
        out_specs=P(None, None, "ka", "slab"),
        check_vma=False,
    )
```

profile of v0, /device:TPU:0, one launch (start us, length us, event | category | flops | bytes accessed | tf_op | source)
XLA Modules:
  0.0 374.2 jit_solution(10600540491712739002)
XLA Ops:
  6.5 3.0 collective-permute-start.5
  12.2 0.8 add_select_fusion.2
  13.0 0.8 compare_and_fusion.1
  13.8 0.8 select_reduce_fusion
  14.6 0.7 fusion.80
  15.3 0.7 fusion.60
  16.0 0.6 fusion.64
  16.6 0.7 fusion.62
  17.4 1.6 fusion.32
  18.9 0.8 fusion.41
  19.7 0.6 fusion.43
  20.4 2.0 collective-permute-start.2
  22.4 1.0 collective-permute-start.1
  23.5 1.5 slice_bitcast_fusion.3
  25.0 8.4 %collective-permute-done.2 = f32[2,1,8,3,16,128]{5,4,3,2,1,0:T(8,128)S(1)} collective-permute-done((f32[2,1,8,3,16,128]{5,4,3,2,1,0:T(8,128)S(1)}, f32[2,1,8,3,16,128]{5,4,3,2,1,0:T(8,128)S(1)}, u32[]{:S(2)}, u32[]{:S(2)}) %collective-permute-start.2) | collective-permute-done | bytes 393248 | tf_op jit(solution)/shard_map/ppermute | solution.py:15
  33.4 7.3 %collective-permute-done.1 = f32[2,1,8,3,16,128]{5,4,3,2,1,0:T(8,128)S(1)} collective-permute-done((f32[2,1,8,3,16,128]{5,4,3,2,1,0:T(8,128)S(1)}, f32[2,1,8,3,16,128]{5,4,3,2,1,0:T(8,128)S(1)}, u32[]{:S(2)}, u32[]{:S(2)}) %collective-permute-start.1) | collective-permute-done | bytes 393248 | tf_op jit(solution)/shard_map/ppermute | solution.py:15
  40.6 0.1 select_select_fusion.1
  40.8 2.6 collective-permute-start.3
  43.4 0.9 fusion.35
  44.3 0.6 integer_pow.17
  44.9 1.8 copy.54
  46.7 3.0 copy.56
  49.7 0.3 fusion.33
  50.0 1.3 broadcast_select_fusion.1
  51.2 0.6 collective-permute-start.7
  51.8 2.3 collective-permute-start.6
  54.2 1.1 select_select_fusion
  55.2 0.8 multiply_subtract_fusion.1
  56.1 0.9 multiply_add_fusion
  57.0 0.8 fusion.7
  57.8 0.8 fusion.49
  58.7 1.7 fusion.6
  60.4 5.9 %copy.73 = f32[16,3,16,256]{0,1,3,2:T(4,128)} copy(f32[16,3,16,256]{3,2,1,0:T(8,128)} %fusion.6) | data formatting | bytes 1572864 | tf_op jit(solution)/shard_map/reshape | solution.py:100
  66.3 48.1 %gather_fusion.1 = f32[6144,16,3]{1,2,0:T(4,128)} fusion(f32[16,3,4096]{0,1,2:T(4,128)} %bitcast.92, s32[6144]{0:T(1024)S(1)} %copy-done.3), kind=kCustom, calls=%fused_computation.1.clone | custom fusion | bytes 2383872 | tf_op jit(solution)/shard_map/jit(_take)/gather | solution.py:106
  114.5 48.4 %gather_fusion = f32[6144,16,3]{1,2,0:T(4,128)} fusion(f32[16,3,4096]{0,1,2:T(4,128)} %bitcast.93, s32[6144]{0:T(1024)S(1)} %copy-done.2), kind=kCustom, calls=%fused_computation.clone | custom fusion | bytes 2383872 | tf_op jit(solution)/shard_map/jit(_take)/gather | solution.py:105
  162.8 46.4 %fusion.1 = (f32[16,6144]{0,1:T(8,128)}, f32[16,6144]{0,1:T(8,128)}) fusion(f32[6144,16,3]{1,2,0:T(4,128)} %gather_fusion.1, f32[6144,16,3]{1,2,0:T(4,128)} %gather_fusion, f32[3,6144]{0,1:T(8,128)} %copy.56, f32[3,6144]{0,1:T(8,128)S(1)} %copy.54, pred[6144]{0:T(1024)(128)(4,1)S(1)} %compare_and_fusion, pred[6144]{0:T(1024)(128)(4,1)S(1)} %get-tuple-element.8), kind=kLoop, calls=%fused_computation.6 | loop fusion | flops 2752512 | bytes 3305472 | tf_op jit(solution)/shard_map/reduce_sum | solution.py:111
  209.3 2.5 copy.57
  211.7 0.8 multiply_bitcast_fusion.1
  212.5 1.1 copy.58
  213.7 2.0 pad_maximum_fusion.1
  215.7 0.6 broadcast_select_fusion.3
  216.3 2.6 collective-permute-start.8
  219.0 1.2 collective-permute-done.9
  220.4 0.1 mul.364
  220.4 0.1 integer_pow.16
  220.6 38.4 %all-reduce.2.cloned.1.call-done = f32[2,16,6144]{2,1,0:T(8,128)} async-done(((f32[2,16,6144]{2,1,0:T(8,128)}), f32[2,16,6144]{2,1,0:T(8,128)}) %all-reduce.2.cloned.1.call-update) | async-done | bytes 786448 | tf_op jit(solution)/shard_map/psum | solution.py:120
  259.0 7.7 %copy.59 = f32[2,16,6144]{1,0,2:T(2,128)} copy(f32[2,16,6144]{2,1,0:T(8,128)} %all-reduce.2.cloned.1.call-done) | data formatting | bytes 1572864 | tf_op jit(solution)/shard_map/psum | solution.py:120
  266.8 9.0 %fusion.81 = bf16[6144,1,2,4,16]{4,3,2,1,0:T(4,128)(2,1)} fusion(f32[16,4]{0,1:T(4,128)S(1)} %divide_multiply_fusion, f32[2,16,6144]{1,0,2:T(2,128)} %copy.59), kind=kLoop, calls=%fused_computation.150 | loop fusion | flops 1572864 | bytes 2359552
  275.8 14.9 %reshape.360 = bf16[8,2,49152]{2,1,0:T(2,128)(2,1)} reshape(bf16[6144,1,2,4,16]{4,3,2,1,0:T(4,128)(2,1)} %fusion.81) | data formatting | bytes 3145728
  290.7 3.7 all-to-all-start
  294.3 0.9 dynamic-slice_convert_fusion
  295.3 0.1 copy.64
  295.4 25.4 %all-gather = bf16[2,128,1536]{2,0,1:T(2,128)(2,1)S(1)} all-gather(bf16[2,16,1536]{2,0,1:T(2,128)(2,1)S(1)} %copy.64), channel_id=2, replica_groups=mesh['ka'=8,'slab'=4] {'ka'}, dimensions={1}, use_global_device_ids=true | all-gather | bytes 884736 | tf_op jit(solution)/shard_map/all_gather | solution.py:127
  320.8 1.0 copy.65
  321.8 10.3 %reshape.361 = bf16[6144,1,2,4,16]{4,3,2,1,0:T(4,128)(2,1)} reshape(bf16[8,2,49152]{2,1,0:T(2,128)(2,1)S(1)} %all-to-all-done) | data formatting | bytes 3145728
  332.1 12.5 %copy.70 = bf16[2,1,16,4,8,768]{5,4,2,3,0,1:T(8,128)(2,1)S(1)} copy(bf16[2,1,16,4,8,768]{2,3,0,5,4,1:T(4,128)(2,1)} %bitcast.91) | data formatting | bytes 3145728 | tf_op jit(solution)/shard_map/all_to_all | solution.py:126
  344.6 0.1 fusion.78
  344.7 0.1 copy.62
  344.9 0.1 copy.61
  345.0 0.1 neg.11
  345.1 0.3 maximum_bitcast_fusion
  345.4 1.9 pad_maximum_fusion
  347.4 3.2 copy.63
  350.6 16.8 %fusion.4 = f32[4,2,768,1536]{3,2,1,0:T(8,128)} fusion(bf16[256,1536,1,1]{1,0,3,2:T(8,128)(2,1)} %bitcast.98, bf16[256,4,2,768]{0,3,2,1:T(8,128)(2,1)S(1)} %copy.63), kind=kOutput, calls=%fused_computation.12 | convolution fusion | flops 4831838208 | bytes 41680896 | tf_op jit(solution)/shard_map/dot_general | solution.py:137
  (37 shorter events, 0.6 us)
Async XLA Ops:
  6.5 37.7 %copy-start.6 = (f32[4]{0:T(128)S(1)}, f32[4]{0:T(128)}, u32[]{:S(2)}) copy-start(f32[4]{0:T(128)} %param.14) | copy-start | bytes 52
  6.5 252.5 %all-reduce.2.cloned.1.call-start = ((), (), s32[]{:S(2)}) async-start(), calls=%async_computation.1 | async-start | bytes 1572864 | tf_op jit(solution)/shard_map/psum | solution.py:120
  6.5 43.4 %collective-permute-start.5 = (f32[1,8]{1,0:T(1,128)}, f32[1,8]{1,0:T(1,128)}, u32[]{:S(2)}, u32[]{:S(2)}) collective-permute-start(f32[1,8]{1,0:T(1,128)} %param.13), channel_id=1, source_target_pairs={{16,0},{20,4},{24,8},{28,12},{0,16},{4,20},{8,24},{12,28},{17,1},{... | collective-permute-start | bytes 104 | tf_op jit(solution)/shard_map/ppermute | solution.py:15
  9.5 10.8 %collective-permute-start = (f32[2,1,8,3,16,128]{5,4,3,2,1,0:T(8,128)}, f32[2,1,8,3,16,128]{5,4,3,2,1,0:T(8,128)S(1)}, u32[]{:S(2)}, u32[]{:S(2)}) collective-permute-start(f32[2,1,8,3,16,128]{5,4,3,2,1,0:T(8,128)} %param.11), channel_id=1, source_target_pairs={{16,0},{20,4},{24,8},{28,12},{0,16},{4,20},{8,24},{12,28},{17,1},{... | collective-permute-start | bytes 1179656 | tf_op jit(solution)/shard_map/ppermute | solution.py:15
  20.4 12.9 %collective-permute-start.2 = (f32[2,1,8,3,16,128]{5,4,3,2,1,0:T(8,128)S(1)}, f32[2,1,8,3,16,128]{5,4,3,2,1,0:T(8,128)S(1)}, u32[]{:S(2)}, u32[]{:S(2)}) collective-permute-start(f32[2,1,8,3,16,128]{5,4,3,2,1,0:T(8,128)S(1)} %broadcast_select_fusion), channel_id=1, source_target_pairs={{24,0},{28,4},{0,8},{4,12},{8,16},{12,20},{16,24},{20,28},{25,1},{... | collective-permute-start | bytes 1179656 | tf_op jit(solution)/shard_map/ppermute | solution.py:15
  22.4 18.2 %collective-permute-start.1 = (f32[2,1,8,3,16,128]{5,4,3,2,1,0:T(8,128)S(1)}, f32[2,1,8,3,16,128]{5,4,3,2,1,0:T(8,128)S(1)}, u32[]{:S(2)}, u32[]{:S(2)}) collective-permute-start(f32[2,1,8,3,16,128]{5,4,3,2,1,0:T(8,128)S(1)} %broadcast_select_fusion), channel_id=1, source_target_pairs={{8,0},{12,4},{16,8},{20,12},{24,16},{28,20},{0,24},{4,28},{9,1},{1... | collective-permute-start | bytes 1179656 | tf_op jit(solution)/shard_map/ppermute | solution.py:15
  40.7 13.5 %collective-permute-start.4 = (f32[2,1,8,3,16,128]{5,4,3,2,1,0:T(8,128)S(1)}, f32[2,1,8,3,16,128]{5,4,3,2,1,0:T(8,128)}, u32[]{:S(2)}, u32[]{:S(2)}) collective-permute-start(f32[2,1,8,3,16,128]{5,4,3,2,1,0:T(8,128)S(1)} %select_select_fusion.1), channel_id=1, source_target_pairs={{28,0},{0,4},{4,8},{8,12},{12,16},{16,20},{20,24},{24,28},{29,1},{... | collective-permute-start | bytes 1179656 | tf_op jit(solution)/shard_map/ppermute | solution.py:15
  40.8 13.4 %collective-permute-start.3 = (f32[2,1,8,3,16,128]{5,4,3,2,1,0:T(8,128)S(1)}, f32[2,1,8,3,16,128]{5,4,3,2,1,0:T(8,128)}, u32[]{:S(2)}, u32[]{:S(2)}) collective-permute-start(f32[2,1,8,3,16,128]{5,4,3,2,1,0:T(8,128)S(1)} %select_select_fusion.1), channel_id=1, source_target_pairs={{4,0},{8,4},{12,8},{16,12},{20,16},{24,20},{28,24},{0,28},{5,1},{9... | collective-permute-start | bytes 1179656 | tf_op jit(solution)/shard_map/ppermute | solution.py:15
  49.7 7.3 %copy-start.1 = (f32[128,128]{1,0:T(8,128)S(1)}, f32[128,128]{1,0:T(8,128)}, u32[]{:S(2)}) copy-start(f32[128,128]{1,0:T(8,128)} %fusion.35) | copy-start | bytes 196612
  51.2 164.4 %collective-permute-start.7 = (f32[1,8]{1,0:T(1,128)}, f32[1,8]{1,0:T(1,128)}, u32[]{:S(2)}, u32[]{:S(2)}) collective-permute-start(f32[1,8]{1,0:T(1,128)} %broadcast_select_fusion.1), channel_id=1, source_target_pairs={{24,0},{28,4},{0,8},{4,12},{8,16},{12,20},{16,24},{20,28},{25,1},{... | collective-permute-start | bytes 104 | tf_op jit(solution)/shard_map/ppermute | solution.py:15
  51.8 163.9 %collective-permute-start.6 = (f32[1,8]{1,0:T(1,128)}, f32[1,8]{1,0:T(1,128)}, u32[]{:S(2)}, u32[]{:S(2)}) collective-permute-start(f32[1,8]{1,0:T(1,128)} %broadcast_select_fusion.1), channel_id=1, source_target_pairs={{8,0},{12,4},{16,8},{20,12},{24,16},{28,20},{0,24},{4,28},{9,1},{1... | collective-permute-start | bytes 104 | tf_op jit(solution)/shard_map/ppermute | solution.py:15
  60.4 5.9 %copy-start.3 = (s32[6144]{0:T(1024)S(1)}, s32[6144]{0:T(1024)}, u32[]{:S(2)}) copy-start(s32[6144]{0:T(1024)} %get-tuple-element.25) | copy-start | bytes 73732
  66.3 48.1 %copy-start.2 = (s32[6144]{0:T(1024)S(1)}, s32[6144]{0:T(1024)}, u32[]{:S(2)}) copy-start(s32[6144]{0:T(1024)} %get-tuple-element.24) | copy-start | bytes 73732
  209.3 3.3 copy-start
  212.5 7.8 %copy-start.5 = (f32[1,2]{1,0:T(1,128)S(1)}, f32[1,2]{1,0:T(1,128)}, u32[]{:S(2)}) copy-start(f32[1,2]{1,0:T(1,128)} %param.12) | copy-start | bytes 28
  212.5 8.0 %copy-start.4 = (f32[4]{0:T(128)S(1)}, f32[4]{0:T(128)}, u32[]{:S(2)}) copy-start(f32[4]{0:T(128)} %integer_pow.17) | copy-start | bytes 52
  216.3 3.9 %collective-permute-start.9 = (f32[1,8]{1,0:T(1,128)S(1)}, f32[1,8]{1,0:T(1,128)S(1)}, u32[]{:S(2)}, u32[]{:S(2)}) collective-permute-start(f32[1,8]{1,0:T(1,128)S(1)} %broadcast_select_fusion.3), channel_id=1, source_target_pairs={{28,0},{0,4},{4,8},{8,12},{12,16},{16,20},{20,24},{24,28},{29,1},{... | collective-permute-start | bytes 104 | tf_op jit(solution)/shard_map/ppermute | solution.py:15
  216.3 3.9 %collective-permute-start.8 = (f32[1,8]{1,0:T(1,128)S(1)}, f32[1,8]{1,0:T(1,128)S(1)}, u32[]{:S(2)}, u32[]{:S(2)}) collective-permute-start(f32[1,8]{1,0:T(1,128)S(1)} %broadcast_select_fusion.3), channel_id=1, source_target_pairs={{4,0},{8,4},{12,8},{16,12},{20,16},{24,20},{28,24},{0,28},{5,1},{9... | collective-permute-start | bytes 104 | tf_op jit(solution)/shard_map/ppermute | solution.py:15
  290.7 31.1 %all-to-all-start = ((bf16[8,2,49152]{2,1,0:T(2,128)(2,1)}), bf16[8,2,49152]{2,1,0:T(2,128)(2,1)S(1)}, u32[]{:S(2)}, u32[]{:S(2)}) async-start(bf16[8,2,49152]{2,1,0:T(2,128)(2,1)} %reshape.360), calls=%async_computation | async-start | bytes 3145728 | tf_op jit(solution)/shard_map/all_to_all | solution.py:126
Sparse Core Ops, SparseCore 0:
  215.8 43.1 all-reduce.1
where the time goes:
time: 376 us; the launch traced here: 374 us
  local copies, waits for them, and re-layouts  164 us (44%)
  other arithmetic  74.8 us (20%)
  waiting for transfers between devices  55.4 us (15%)
  blocking collectives  25.4 us (7%)
  matrix products  20.2 us (5%)
  starting transfers between devices  18 us (5%)
  between operations  16.3 us (4%)
    gather x1, local copies, waits for them, and re-layouts, per_device(): part_re = jnp.take(flat, column, axis=2)  48.4 us
    gather x1, local copies, waits for them, and re-layouts, per_device(): part_im = jnp.take(flat, column + extent_z, axis=2)  48.1 us
    reduce_sum x1, other arithmetic, per_device(): pair_re = jnp.sum(part_re * xcos + part_im * xsin, axis=1) * norm  46.4 us
    psum x1, waiting for transfers between devices, per_device(): whole = lax.psum(partial_value, 'slab')  38.4 us
    all_gather x1, blocking collectives, per_device(): columns = lax.all_gather(column_side[:, None], 'ka', axis=1, tiled=True)  25.4 us
    unnamed x16, local copies, waits for them, and re-layouts  25.2 us
    ppermute x10, waiting for transfers between devices, passed_along(): return lax.ppermute(block, axis, route)  17 us
    dot_general x1, matrix products, per_device(): lax.dot_general(left, right, (((0,), (0,)), ((), ())), preferred_element_...  16.8 us
  transfers between devices with their start and end apart: 12, of which 4 were waited for; matrix products, arithmetic and copies ran while one was open for 49% of the time, Pallas kernels for 0%

commit v1 on v0

v1 whole, which is shorter than its diff:
```python
import functools
import math

import jax
import jax.numpy as jnp
import numpy as np
from jax import lax
from jax.experimental import pallas as pl
from jax.experimental.pallas import tpu as pltpu
from jax.sharding import PartitionSpec as P

two_pi = 2.0 * math.pi
f32 = jnp.float32
bf16 = jnp.bfloat16


def halves(table):
    high = table.astype(np.float32).astype(bf16)
    low = (table - high.astype(np.float64)).astype(np.float32).astype(bf16)
    return jnp.asarray(np.stack([high, low]))


def dft_angle(length):
    index = np.arange(length)
    return two_pi * (index[:, None] * index[None, :] % length) / length


def z_table(length):
    angle = dft_angle(length)
    cosine, sine = np.cos(angle), np.sin(angle)
    return halves(np.block([[cosine, sine], [-sine, cosine]]))


def plane_table(extent_x, extent_y):
    angle = np.kron(dft_angle(extent_x), np.ones((extent_y, extent_y))) + np.kron(
        np.ones((extent_x, extent_x)), dft_angle(extent_y)
    )
    return halves(np.cos(angle)), halves(np.sin(angle))


def split(value):
    high = value.astype(bf16)
    return high, (value - high.astype(f32)).astype(bf16)


def dot(a, b, dims):
    return lax.dot_general(a, b, (dims, ((), ())), preferred_element_type=f32)


def dot3(a, b, dims):
    return dot(a[0], b[0], dims) + dot(a[1], b[0], dims) + dot(a[0], b[1], dims)


def pair_kernel(norm, tile, val, cond, ztab, ctab, stab, gxy, gz, out, spectrum):
    bands_v, bands_c = val.shape[1], cond.shape[1]
    points, length = val.shape[2], val.shape[3]
    pairs = bands_v * bands_c
    ztable = (ztab[0], ztab[1])
    ctable = (ctab[0], ctab[1])
    stable = (stab[0], stab[1])
    for v in range(bands_v):
        for c in range(bands_c):
            p = v * bands_c + c
            re = val[0, v] * cond[0, c] + val[1, v] * cond[1, c]
            im = val[0, v] * cond[1, c] - val[1, v] * cond[0, c]
            field = split(jnp.concatenate([re, im], axis=1))
            along = split(dot3(ztable, field, ((1,), (1,))))
            even = dot3(along, ctable, ((1,), (0,)))
            odd = dot3(along, stable, ((1,), (0,)))
            real = (even[:length] + odd[length:]) * norm
            imag = (even[length:] - odd[:length]) * norm
            spectrum[pl.ds(p * length, length), :] = real.astype(bf16)
            spectrum[pl.ds((pairs + p) * length, length), :] = imag.astype(bf16)

    @pl.loop(0, out.shape[1] // tile)
    def _(step):
        cols = pl.ds(pl.multiple_of(step * tile, tile), tile)
        chosen = lax.broadcasted_iota(jnp.int32, (points, tile), 0) == gxy[:, cols]
        picked = dot(spectrum[...], chosen.astype(f32).astype(bf16), ((1,), (0,)))
        here = lax.broadcasted_iota(jnp.int32, (length, tile), 0) == gz[:, cols]
        rows = [
            jnp.sum(
                jnp.where(here, picked[r * length : (r + 1) * length], 0.0),
                axis=0,
                keepdims=True,
            )
            for r in range(2 * pairs)
        ]
        out[:, cols] = jnp.concatenate(rows, axis=0).astype(bf16)


def make_pairs(val, cond, gxy, gz, norm, tables):
    bands_v, bands_c = val.shape[1], cond.shape[1]
    points, length = val.shape[2], val.shape[3]
    total = gxy.shape[1]
    rows = 2 * bands_v * bands_c
    tile = 512 if total % 512 == 0 else 128
    vmem = pl.BlockSpec(memory_space=pltpu.VMEM)
    return pl.pallas_call(
        functools.partial(pair_kernel, norm, tile),
        out_shape=jax.ShapeDtypeStruct((rows, total), bf16),
        in_specs=[vmem] * 7,
        out_specs=vmem,
        scratch_shapes=[pltpu.VMEM((rows * length, points), bf16)],
        cost_estimate=pl.CostEstimate(
            flops=2 * rows * length * points * total, bytes_accessed=1 << 21, transcendentals=0
        ),
        name="pairs",
    )(val, cond, *tables, gxy, gz)


def product_kernel(tile, rows, cols, wsame, wswap, out, same, swap):
    @pl.when((pl.program_id(0) == 0) & (pl.program_id(1) == 0))
    def _():
        depth, width = rows.shape
        wide = rows[...].astype(f32)
        same[...] = wide.T
        group = wide.reshape(depth // 8, 8, width)
        turned = jnp.concatenate([group[:, 4:], group[:, :4]], axis=1)
        swap[...] = turned.reshape(depth, width).T

    step = pl.program_id(1)
    here = pl.ds(pl.multiple_of(step * tile, tile), tile)
    weight_same = wsame[pl.ds(pl.program_id(0), 1), :]
    weight_swap = wswap[pl.ds(pl.program_id(0), 1), :]
    right = cols[...]
    out[0, 0] = dot((same[here, :] * weight_same).astype(bf16), right, ((1,), (0,)))
    out[0, 1] = dot((swap[here, :] * weight_swap).astype(bf16), right, ((1,), (0,)))


def make_product(rows, cols, wsame, wswap):
    depth, height = rows.shape
    width = cols.shape[1]
    freqs = wsame.shape[0]
    tile = 128 if height % 128 == 0 else height
    vmem = pl.BlockSpec(memory_space=pltpu.VMEM)
    return pl.pallas_call(
        functools.partial(product_kernel, tile),
        out_shape=jax.ShapeDtypeStruct((freqs, 2, height, width), f32),
        grid=(freqs, height // tile),
        in_specs=[vmem] * 4,
        out_specs=pl.BlockSpec((1, 2, tile, width), lambda w, t: (w, 0, t, 0)),
        scratch_shapes=[pltpu.VMEM((height, depth), f32)] * 2,
        cost_estimate=pl.CostEstimate(
            flops=4 * freqs * depth * height * width,
            bytes_accessed=8 * freqs * height * width,
            transcendentals=0,
        ),
        name="product",
    )(rows, cols, wsame, wswap)


def route(payload, shift_flat, grid_side, count):
    for grid_dim in range(3):
        stride = grid_side ** (2 - grid_dim)
        for bit_pos in range(grid_side.bit_length() - 1):
            hop = 1 << bit_pos
            perm = []
            for source in range(count):
                coord = source // stride % grid_side
                perm.append((source, source + ((coord + hop) % grid_side - coord) * stride))
            moved = lax.ppermute(payload, "ka", perm)
            chosen = shift_flat // stride % grid_side // hop % 2 == 1
            payload = jnp.where(chosen, moved, payload)
    return payload


def per_device(
    val_wave, cond_wave, val_energy, cond_energy, frequency, kpoint_map, umklapp, gvector_index
):
    slab_count = lax.axis_size("slab")
    kpoint_count = lax.axis_size("ka")
    kpoint_here = lax.axis_index("ka")
    slab_here = lax.axis_index("slab")
    grid_side = max((candidate for candidate in range(1, 9) if candidate**3 <= kpoint_count))
    bands_v, planes, extent_y, extent_z = val_wave.shape[2:]
    bands_c = cond_wave.shape[2]
    extent_x = planes * slab_count
    local_c = bands_c // slab_count
    total_g = gvector_index.shape[0]
    points = extent_x * extent_y

    cond = lax.all_to_all(cond_wave[:, 0], "slab", split_axis=1, concat_axis=2, tiled=True)

    index = jnp.arange(kpoint_count, dtype=jnp.int32)
    shift_vec = jnp.sum(jnp.where(index[None, :] == kpoint_here, umklapp, 0), axis=1)
    xpos = slab_here * planes + jnp.arange(planes, dtype=jnp.int32)
    ypos = jnp.arange(extent_y, dtype=jnp.int32)
    zpos = jnp.arange(extent_z, dtype=jnp.int32)
    first_part = (shift_vec[0] * xpos % extent_x).astype(f32)[:, None, None] / extent_x
    second_part = (shift_vec[1] * ypos % extent_y).astype(f32)[None, :, None] / extent_y
    third_part = (shift_vec[2] * zpos % extent_z).astype(f32)[None, None, :] / extent_z
    angle = two_pi * (first_part + second_part + third_part)
    cosine = jnp.cos(angle)
    sine = jnp.sin(angle)
    val_re, val_im = val_wave[0, 0], val_wave[1, 0]
    turned = jnp.stack([val_re * cosine + val_im * sine, val_im * cosine - val_re * sine])
    routed = route(turned, kpoint_map[0], grid_side, kpoint_count)
    val = lax.all_gather(routed, "slab", axis=2, tiled=True)

    tables = (z_table(extent_z), *plane_table(extent_x, extent_y))
    norm = 1.0 / (2.0 * math.sqrt(points * extent_z))
    pair_low = make_pairs(
        val.reshape(2, bands_v, points, extent_z),
        cond.reshape(2, local_c, points, extent_z),
        (gvector_index // extent_z)[None],
        (gvector_index % extent_z)[None],
        norm,
        tables,
    )
    part = pair_low.shape[0]

    columns = lax.all_to_all(
        pair_low, "slab", split_axis=1, concat_axis=0, tiled=True
    )
    columns = lax.all_gather(columns, "ka", axis=0, tiled=True)
    rows = lax.all_to_all(
        pair_low.reshape(part, kpoint_count, total_g // kpoint_count),
        "ka", split_axis=1, concat_axis=0, tiled=True,
    ).reshape(kpoint_count, part, total_g // kpoint_count)
    rows = lax.all_gather(rows, "slab", axis=1, tiled=True)
    depth = kpoint_count * slab_count * part
    rows = rows.reshape(depth, total_g // kpoint_count)

    energies = lax.all_gather(
        jnp.concatenate([val_energy, cond_energy], axis=1), "ka", axis=0, tiled=True
    )
    came = kpoint_map[None, :] == index[:, None]
    val_level = jnp.sum(
        jnp.where(came[:, :, None], energies[None, :, :bands_v], 0.0), axis=1
    )
    cond_level = energies[:, bands_v:].reshape(kpoint_count, slab_count, 1, local_c)
    gap = val_level[:, None, :, None] - cond_level
    gap = gap.reshape(kpoint_count * slab_count, 1, bands_v * local_c)
    freq = frequency[:, None, None, None]
    weight = 2.0 * gap[None] / (gap[None] ** 2 + freq**2) / kpoint_count
    wsame = jnp.concatenate([weight, weight], axis=2).reshape(-1, depth)
    wswap = jnp.concatenate([weight, -weight], axis=2).reshape(-1, depth)
    return make_product(rows, columns, wsame, wswap)


def solution(mesh):
    return jax.shard_map(
        per_device,
        mesh=mesh,
        in_specs=(
            P(None, "ka", None, "slab", None, None),
            P(None, "ka", None, "slab", None, None),
            P("ka", None),
            P("ka", None),
            P(),
            P(),
            P(),
            P(),
        ),
        out_specs=P(None, None, "ka", "slab"),
        check_vma=False,
    )
```

time: 376 us -> 122 us (0.32)
  local copies, waits for them, and re-layouts: 164 us -> 5.55 us
  other arithmetic: 74.8 us -> 7.63 us
  waiting for transfers between devices: 55.4 us -> 7.99 us
  Pallas kernels: 0 us -> 29.5 us
  blocking collectives: 25.4 us -> 50.9 us
  matrix products: 20.2 us -> 0 us
  between operations: 16.3 us -> 2.73 us
    gather x2 -> x0, local copies, waits for them, and re-layouts: 96.5 us -> none  [the longest x1 48.4 us: per_device(): part_re = jnp.take(flat, column, axis=2)]
    reduce_sum x2, other arithmetic: 47.2 us -> 0.88 us  [the longest x1 0.8 us: per_device(): jnp.sum(jnp.where(index[None, :] == kpoint_here, umklapp, 0), axis=1)]
    psum x1 -> x0, waiting for transfers between devices: 38.4 us -> none  [per_device(): whole = lax.psum(partial_value, 'slab')]
    pallas_call x0 -> x2, Pallas kernels: none -> 29.5 us  [the longest x1 20.2 us: make_product(): pl.pallas_call(functools.partial(product_kernel, tile), out_shape=jax.Sha...]
    all_gather x1 -> x4, blocking collectives: 25.4 us -> 50.9 us  [the longest x1 15.9 us: per_device(): val = lax.all_gather(routed, 'slab', axis=2, tiled=True)]
    unnamed x16 -> x1, local copies, waits for them, and re-layouts: 25.2 us -> 1.78 us
    dot_general x4 -> x0, matrix products: 20.2 us -> none  [the longest x1 16.8 us: per_device(): lax.dot_general(left, right, (((0,), (0,)), ((), ())), preferred_element_...]
    ppermute x10 -> x3, waiting for transfers between devices: 17 us -> 4.75 us  [route(): moved = lax.ppermute(payload, 'ka', perm)]
  transfers between devices with their start and end apart: 12 -> 6, of which waited for: 4 -> 3; matrix products, arithmetic and copies ran while one was open for 49% -> 7% of each run, Pallas kernels for 0% -> 0%
where the time goes in v1:
time: 122 us; the launch traced here: 121 us
  blocking collectives  50.9 us (42%)
  Pallas kernels  29.5 us (24%)
  starting transfers between devices  17 us (14%)
  waiting for transfers between devices  7.99 us (7%)
  other arithmetic  7.63 us (6%)
  local copies, waits for them, and re-layouts  5.55 us (5%)
  between operations  2.73 us (2%)
    pallas_call x1, Pallas kernels, make_product(): pl.pallas_call(functools.partial(product_kernel, tile), out_shape=jax.Sha...  20.2 us
    all_gather x1, blocking collectives, per_device(): val = lax.all_gather(routed, 'slab', axis=2, tiled=True)  15.9 us
    all_gather x1, blocking collectives, per_device(): rows = lax.all_gather(rows, 'slab', axis=1, tiled=True)  15.6 us
    all_gather x1, blocking collectives, per_device(): columns = lax.all_gather(columns, 'ka', axis=0, tiled=True)  10.7 us
    pallas_call x1, Pallas kernels, make_pairs(): pl.pallas_call(functools.partial(pair_kernel, norm, tile), out_shape=jax....  9.24 us
    all_gather x1, blocking collectives, per_device(): lax.all_gather(jnp.concatenate([val_energy, cond_energy], axis=1), 'ka',...  8.75 us
    all_to_all x1, starting transfers between devices, per_device(): lax.all_to_all(pair_low, 'slab', split_axis=1, concat_axis=0, tiled=True)  5.08 us
    all_to_all x1, starting transfers between devices, per_device(): lax.all_to_all(cond_wave[:, 0], 'slab', split_axis=1, concat_axis=2, tile...  4.87 us
  transfers between devices with their start and end apart: 6, of which 3 were waited for; matrix products, arithmetic and copies ran while one was open for 7% of the time, Pallas kernels for 0%

profile of v1, /device:TPU:0, one launch (start us, length us, event | category | flops | bytes accessed | tf_op | source)
XLA Modules:
  0.0 121.3 jit_solution(1358519920368492377)
XLA Ops:
  0.0 0.8 select_reduce_fusion.1
  0.8 0.7 fusion.15
  1.5 0.6 fusion.11
  2.1 0.6 fusion.9
  2.7 0.7 fusion.7
  3.4 0.1 broadcast_add_fusion
  3.5 0.2 fusion.3
  3.7 0.8 fusion
  4.5 3.1 %collective-permute-start = (f32[2,2,3,16,128]{4,3,2,1,0:T(8,128)S(1)}, f32[2,2,3,16,128]{4,3,2,1,0:T(8,128)S(1)}, u32[]{:S(2)}, u32[]{:S(2)}) collective-permute-start(f32[2,2,3,16,128]{4,3,2,1,0:T(8,128)S(1)} %pad_maximum_fusion), channel_id=1, source_target_pairs={{0,16},{4,20},{8,24},{12,28},{16,0},{20,4},{24,8},{28,12},{1,17},{... | collective-permute-start | bytes 294920 | tf_op jit(solution)/shard_map/ppermute | solution.py:162
  7.6 1.8 %copy.36 = f32[2,1,8,3,16,128]{5,4,3,0,2,1:T(8,128)} copy(f32[2,1,8,3,16,128]{5,4,3,2,1,0:T(8,128)} %param.12) | data formatting | bytes 786432 | tf_op args[1]
  9.4 4.9 %all-to-all-start = ((f32[2,8,3,16,128]{4,3,2,0,1:T(8,128)}), f32[2,8,3,16,128]{4,3,2,0,1:T(8,128)S(1)}, u32[]{:S(2)}, u32[]{:S(2)}) async-start(f32[2,8,3,16,128]{4,3,2,0,1:T(8,128)} %bitcast.48), calls=%async_computation | async-start | bytes 786432 | tf_op jit(solution)/shard_map/all_to_all | solution.py:183
  16.9 0.7 iota_compare_fusion
  17.5 0.7 maximum_bitcast_fusion
  18.3 8.8 %all-gather.1 = f32[8,1,10]{2,1,0:T(1,128)S(1)} all-gather(f32[1,1,10]{2,1,0:T(1,128)S(1)} %maximum_bitcast_fusion), channel_id=1, replica_groups=mesh['ka'=8,'slab'=4] {'ka'}, dimensions={0}, use_global_device_ids=true | all-gather | bytes 360 | tf_op jit(solution)/shard_map/all_gather | solution.py:225
  27.0 0.1 slice.31
  27.1 0.1 copy.30
  27.2 0.1 copy.31
  27.2 0.1 copy.32
  27.3 1.4 %add_select_fusion = (s32[6144]{0:T(1024)}, s32[6144]{0:T(1024)}) fusion(s32[6144]{0:T(1024)} %param.18), kind=kLoop, calls=%fused_computation.11 | loop fusion | flops 116736 | bytes 73728 | tf_op jit(solution)/shard_map/jit(remainder)/select_n | solution.py:207
  28.7 0.1 select_reduce_fusion
  28.8 0.0 collective-permute-done
  28.8 0.6 collective-permute-start.1
  29.4 0.1 subtract_multiply_fusion.1
  29.5 0.7 integer_pow.17
  30.2 0.1 mul.133
  30.3 0.1 integer_pow.16
  30.4 3.5 %collective-permute-done.1 = f32[2,2,3,16,128]{4,3,2,1,0:T(8,128)S(1)} collective-permute-done((f32[2,2,3,16,128]{4,3,2,1,0:T(8,128)S(1)}, f32[2,2,3,16,128]{4,3,2,1,0:T(8,128)S(1)}, u32[]{:S(2)}, u32[]{:S(2)}) %collective-permute-start.1) | collective-permute-done | bytes 98336 | tf_op jit(solution)/shard_map/ppermute | solution.py:162
  33.9 0.1 collective-permute-start.2
  34.0 0.1 fusion.14
  34.1 1.2 collective-permute-done.2
  35.3 15.9 %all_gather.12 = f32[2,2,12,16,128]{4,3,2,1,0:T(8,128)} all-gather(f32[2,2,3,16,128]{4,3,2,1,0:T(8,128)S(1)} %broadcast_select_fusion.2), channel_id=1, replica_groups=mesh['ka'=8,'slab'=4] {'slab'}, dimensions={2}, use_global_device_ids=true | all-gather | bytes 491520 | tf_op jit(solution)/shard_map/all_gather | solution.py:199
  51.2 0.0 all-to-all-done
  51.2 0.8 copy.29
  52.0 9.2 %pairs.1 = bf16[8,6144]{1,0:T(8,128)(2,1)} custom-call(f32[2,2,192,128]{3,2,1,0:T(8,128)} %bitcast.57, f32[2,2,192,128]{3,2,1,0:T(8,128)} %bitcast.53, bf16[2,256,256]{2,1,0:T(8,128)(2,1)} %constant.177.clone.ztab, bf16[2,192,192]{2,1,0:T(8,128)(2,1)} %constant.178.clone.ctab, bf16[2,192,192]{2,1,0:T(8,128)(2,1)} %constant.179.clone.stab, ...), custom_call_target="tpu_custom_call" | custom-call | flops 2415919104 | bytes 2097152 | tf_op jit(solution)/shard_map/pairs/pallas_call | solution.py:99
  61.2 3.4 %all-to-all-start.1 = ((bf16[8,8,768]{2,0,1:T(8,128)(2,1)}), bf16[8,8,768]{2,0,1:T(8,128)(2,1)S(1)}, u32[]{:S(2)}, u32[]{:S(2)}) async-start(bf16[8,8,768]{2,0,1:T(8,128)(2,1)} %bitcast.54), calls=%async_computation.1 | async-start | bytes 196608 | tf_op jit(solution)/shard_map/all_to_all | solution.py:217
  64.6 0.1 copy.34
  64.7 0.8 reshape.244.wswap
  65.5 0.1 copy.33
  65.7 0.8 reshape.243.wsame
  66.5 3.2 %all-to-all-done.1 = bf16[8,8,768]{2,0,1:T(8,128)(2,1)S(1)} async-done(((bf16[8,8,768]{2,0,1:T(8,128)(2,1)}), bf16[8,8,768]{2,0,1:T(8,128)(2,1)S(1)}, u32[]{:S(2)}, u32[]{:S(2)}) %all-to-all-start.1) | async-done | bytes 98336 | tf_op jit(solution)/shard_map/all_to_all | solution.py:217
  69.7 5.1 %all-to-all-start.2 = ((bf16[8,4,1536]{2,0,1:T(8,128)(2,1)}), bf16[8,4,1536]{2,0,1:T(8,128)(2,1)S(1)}, u32[]{:S(2)}, u32[]{:S(2)}) async-start(bf16[8,4,1536]{2,0,1:T(8,128)(2,1)} %bitcast.55), calls=%async_computation.2 | async-start | bytes 196608 | tf_op jit(solution)/shard_map/all_to_all | solution.py:213
  74.8 15.6 %all-gather = bf16[8,32,1,768]{3,1,0,2:T(8,128)(2,1)} all-gather(bf16[8,8,1,768]{3,1,0,2:T(8,128)(2,1)S(1)} %bitcast.58), channel_id=2, replica_groups=mesh['ka'=8,'slab'=4] {'slab'}, dimensions={1}, use_global_device_ids=true | all-gather | bytes 491520 | tf_op jit(solution)/shard_map/all_gather | solution.py:221
  90.4 0.0 all-to-all-done.2
  90.4 10.7 %all_gather.14.cols = bf16[256,1536]{1,0:T(8,128)(2,1)} all-gather(bf16[32,1536]{1,0:T(8,128)(2,1)S(1)} %bitcast.56), channel_id=1, replica_groups=mesh['ka'=8,'slab'=4] {'ka'}, dimensions={0}, use_global_device_ids=true | all-gather | bytes 884736 | tf_op jit(solution)/shard_map/all_gather | solution.py:216
  101.1 20.2 %product.1 = f32[4,2,768,1536]{3,2,1,0:T(8,128)} custom-call(bf16[256,768]{1,0:T(8,128)(2,1)} %bitcast.51, bf16[256,1536]{1,0:T(8,128)(2,1)} %all_gather.14.cols, f32[4,256]{1,0:T(4,128)} %reshape.243.wsame, f32[4,256]{1,0:T(4,128)} %reshape.244.wswap), custom_call_target="tpu_custom_call" | custom-call | flops 4831838208 | bytes 37748736 | tf_op jit(solution)/shard_map/product/pallas_call | solution.py:137
  (6 shorter events, 0.1 us)
Async XLA Ops:
  4.5 24.3 %collective-permute-start = (f32[2,2,3,16,128]{4,3,2,1,0:T(8,128)S(1)}, f32[2,2,3,16,128]{4,3,2,1,0:T(8,128)S(1)}, u32[]{:S(2)}, u32[]{:S(2)}) collective-permute-start(f32[2,2,3,16,128]{4,3,2,1,0:T(8,128)S(1)} %pad_maximum_fusion), channel_id=1, source_target_pairs={{0,16},{4,20},{8,24},{12,28},{16,0},{20,4},{24,8},{28,12},{1,17},{... | collective-permute-start | bytes 294920 | tf_op jit(solution)/shard_map/ppermute | solution.py:162
  9.4 41.8 %all-to-all-start = ((f32[2,8,3,16,128]{4,3,2,0,1:T(8,128)}), f32[2,8,3,16,128]{4,3,2,0,1:T(8,128)S(1)}, u32[]{:S(2)}, u32[]{:S(2)}) async-start(f32[2,8,3,16,128]{4,3,2,0,1:T(8,128)} %bitcast.48), calls=%async_computation | async-start | bytes 786432 | tf_op jit(solution)/shard_map/all_to_all | solution.py:183
  28.8 5.1 %collective-permute-start.1 = (f32[2,2,3,16,128]{4,3,2,1,0:T(8,128)S(1)}, f32[2,2,3,16,128]{4,3,2,1,0:T(8,128)S(1)}, u32[]{:S(2)}, u32[]{:S(2)}) collective-permute-start(f32[2,2,3,16,128]{4,3,2,1,0:T(8,128)S(1)} %broadcast_select_fusion), channel_id=1, source_target_pairs={{0,8},{4,12},{8,0},{12,4},{16,24},{20,28},{24,16},{28,20},{1,9},{5... | collective-permute-start | bytes 294920 | tf_op jit(solution)/shard_map/ppermute | solution.py:162
  33.9 1.4 %collective-permute-start.2 = (f32[2,2,3,16,128]{4,3,2,1,0:T(8,128)S(1)}, f32[2,2,3,16,128]{4,3,2,1,0:T(8,128)S(1)}, u32[]{:S(2)}, u32[]{:S(2)}) collective-permute-start(f32[2,2,3,16,128]{4,3,2,1,0:T(8,128)S(1)} %broadcast_select_fusion.1), channel_id=1, source_target_pairs={{0,4},{4,0},{8,12},{12,8},{16,20},{20,16},{24,28},{28,24},{1,5},{5... | collective-permute-start | bytes 294920 | tf_op jit(solution)/shard_map/ppermute | solution.py:162
  61.2 8.5 %all-to-all-start.1 = ((bf16[8,8,768]{2,0,1:T(8,128)(2,1)}), bf16[8,8,768]{2,0,1:T(8,128)(2,1)S(1)}, u32[]{:S(2)}, u32[]{:S(2)}) async-start(bf16[8,8,768]{2,0,1:T(8,128)(2,1)} %bitcast.54), calls=%async_computation.1 | async-start | bytes 196608 | tf_op jit(solution)/shard_map/all_to_all | solution.py:217
  69.7 20.7 %all-to-all-start.2 = ((bf16[8,4,1536]{2,0,1:T(8,128)(2,1)}), bf16[8,4,1536]{2,0,1:T(8,128)(2,1)S(1)}, u32[]{:S(2)}, u32[]{:S(2)}) async-start(bf16[8,4,1536]{2,0,1:T(8,128)(2,1)} %bitcast.55), calls=%async_computation.2 | async-start | bytes 196608 | tf_op jit(solution)/shard_map/all_to_all | solution.py:213

commit v2 on v1

v2 whole, which is shorter than its diff:
```python
import functools
import math

import jax
import jax.numpy as jnp
import numpy as np
from jax import lax
from jax.experimental import pallas as pl
from jax.experimental.pallas import tpu as pltpu
from jax.sharding import PartitionSpec as P

two_pi = 2.0 * math.pi
f32 = jnp.float32
bf16 = jnp.bfloat16


def halves(table):
    high = table.astype(np.float32).astype(bf16)
    low = (table - high.astype(np.float64)).astype(np.float32).astype(bf16)
    return jnp.asarray(np.stack([high, low]))


def dft_angle(length):
    index = np.arange(length)
    return two_pi * (index[:, None] * index[None, :] % length) / length


def z_table(length):
    angle = dft_angle(length)
    cosine, sine = np.cos(angle), np.sin(angle)
    return halves(np.block([[cosine, sine], [-sine, cosine]]))


def plane_table(extent_x, extent_y):
    angle = np.kron(dft_angle(extent_x), np.ones((extent_y, extent_y))) + np.kron(
        np.ones((extent_x, extent_x)), dft_angle(extent_y)
    )
    return halves(np.cos(angle)), halves(np.sin(angle))


def split(value):
    high = value.astype(bf16)
    return high, (value - high.astype(f32)).astype(bf16)


def dot(a, b, dims):
    return lax.dot_general(a, b, (dims, ((), ())), preferred_element_type=f32)


def dot3(a, b, dims):
    return dot(a[0], b[0], dims) + dot(a[1], b[0], dims) + dot(a[0], b[1], dims)


def pair_kernel(norm, val, cond, ztab, ctab, stab, gxy, gz, out, spectrum):
    blocks, _, bands_v, _, length = val.shape
    bands_c = cond.shape[2]
    pairs = bands_v * bands_c
    points = spectrum.shape[1]
    tile = out.shape[2]
    ztable = (ztab[0], ztab[1])
    ctable = (ctab[0], ctab[1])
    stable = (stab[0], stab[1])
    for v in range(bands_v):
        for c in range(bands_c):
            p = v * bands_c + c
            pieces = []
            for b in range(blocks):
                val_re, val_im = val[b, 0, v], val[b, 1, v]
                cond_re, cond_im = cond[b, 0, c], cond[b, 1, c]
                re = val_re * cond_re + val_im * cond_im
                im = val_re * cond_im - val_im * cond_re
                pieces.append(jnp.concatenate([re, im], axis=1))
            field = split(jnp.concatenate(pieces, axis=0))
            along = split(dot3(ztable, field, ((1,), (1,))))
            even = dot3(along, ctable, ((1,), (0,)))
            odd = dot3(along, stable, ((1,), (0,)))
            real = (even[:length] + odd[length:]) * norm
            imag = (even[length:] - odd[:length]) * norm
            spectrum[pl.ds(p * length, length), :] = real.astype(bf16)
            spectrum[pl.ds((pairs + p) * length, length), :] = imag.astype(bf16)

    @pl.loop(0, out.shape[0])
    def _(step):
        cols = pl.ds(pl.multiple_of(step * tile, tile), tile)
        chosen = lax.broadcasted_iota(jnp.int32, (points, tile), 0) == gxy[:, cols]
        picked = dot(spectrum[...], chosen.astype(f32).astype(bf16), ((1,), (0,)))
        here = lax.broadcasted_iota(jnp.int32, (length, tile), 0) == gz[:, cols]
        rows = [
            jnp.sum(
                jnp.where(here, picked[r * length : (r + 1) * length], 0.0),
                axis=0,
                keepdims=True,
            )
            for r in range(2 * pairs)
        ]
        out[step] = jnp.concatenate(rows, axis=0).astype(bf16)


def make_pairs(val, cond, gxy, gz, tile, norm, tables):
    blocks, _, bands_v, rows, length = val.shape
    bands_c = cond.shape[2]
    points = blocks * rows
    total = gxy.shape[1]
    part = 2 * bands_v * bands_c
    vmem = pl.BlockSpec(memory_space=pltpu.VMEM)
    return pl.pallas_call(
        functools.partial(pair_kernel, norm),
        out_shape=jax.ShapeDtypeStruct((total // tile, part, tile), bf16),
        in_specs=[vmem] * 7,
        out_specs=vmem,
        scratch_shapes=[pltpu.VMEM((part * length, points), bf16)],
        cost_estimate=pl.CostEstimate(
            flops=2 * part * length * points * total, bytes_accessed=1 << 21, transcendentals=0
        ),
        name="pairs",
    )(val, cond, *tables, gxy, gz)


def meet(peers):
    barrier = pltpu.get_barrier_semaphore()
    for peer in peers:
        pl.semaphore_signal(barrier, inc=1, device_id=peer, device_id_type=pl.DeviceIdType.MESH)
    pl.semaphore_wait(barrier, len(peers))


def others(count_ka, count_slab):
    k, s = lax.axis_index("ka"), lax.axis_index("slab")
    along_ka = [(lax.rem(k + d, count_ka), s) for d in range(1, count_ka)]
    along_slab = [(k, lax.rem(s + d, count_slab)) for d in range(1, count_slab)]
    return k, s, along_ka, along_slab


def send(source, target, sems, number, peer):
    copy = pltpu.make_async_remote_copy(
        src_ref=source,
        dst_ref=target,
        send_sem=sems[0].at[number],
        recv_sem=sems[1].at[number],
        device_id=peer,
        device_id_type=pl.DeviceIdType.MESH,
    )
    copy.start()
    return copy


def keep(source, target, sem):
    copy = pltpu.make_async_copy(source, target, sem)
    copy.start()
    return copy


def spread_kernel(counts, val, cond, level, val_all, cond_all, level_all, sa, ra, sb, rb, sc, rc, own):
    k, s, along_ka, along_slab = others(*counts)
    meet(along_ka + along_slab)
    copies = []
    for i, peer in enumerate(along_ka):
        copies.append(send(val, val_all.at[k], (sa, ra), i, peer))
    for i, peer in enumerate(along_slab):
        copies.append(send(cond.at[peer[1]], cond_all.at[s], (sb, rb), i, peer))
    for i, peer in enumerate(along_ka):
        copies.append(send(level, level_all.at[k], (sc, rc), i, peer))
    copies.append(keep(val, val_all.at[k], own.at[0]))
    copies.append(keep(cond.at[s], cond_all.at[s], own.at[1]))
    copies.append(keep(level, level_all.at[k], own.at[2]))
    for copy in copies:
        copy.wait()


def gather_kernel(counts, val, val_all, sa, ra, own):
    k, s, _, along_slab = others(*counts)
    meet(along_slab)
    copies = [
        send(val, val_all.at[s], (sa, ra), i, peer) for i, peer in enumerate(along_slab)
    ]
    copies.append(keep(val, val_all.at[s], own.at[0]))
    for copy in copies:
        copy.wait()


def share_kernel(counts, tiles, blocks, cols_all, rows_all, sa, ra, sb, rb, sc, rc, sd, rd, own):
    k, s, along_ka, along_slab = others(*counts)
    per_column = cols_all.shape[0]
    meet(along_ka + along_slab)
    mine = [keep(blocks.at[k], rows_all.at[s, k], own.at[0])]
    mine.append(
        keep(tiles.at[pl.ds(s * per_column, per_column)], cols_all.at[:, s, k], own.at[1])
    )
    row_first = [
        send(blocks.at[peer[0]], rows_all.at[s, k], (sa, ra), i, peer)
        for i, peer in enumerate(along_ka)
    ]
    col_first = [
        send(
            tiles.at[pl.ds(peer[1] * per_column, per_column)],
            cols_all.at[:, s, k], (sb, rb), i, peer,
        )
        for i, peer in enumerate(along_slab)
    ]
    for copy in mine:
        copy.wait()
    for copy in row_first:
        copy.wait_recv()
    row_next = [
        send(rows_all.at[s], rows_all.at[s], (sc, rc), i, peer)
        for i, peer in enumerate(along_slab)
    ]
    for copy in col_first:
        copy.wait_recv()
    col_next = [
        send(cols_all.at[:, :, k], cols_all.at[:, :, k], (sd, rd), i, peer)
        for i, peer in enumerate(along_ka)
    ]
    for copy in row_first + col_first:
        copy.wait_send()
    for copy in row_next + col_next:
        copy.wait()


def exchange(body, name, number, counts, operands, outs, lanes):
    vmem = pl.BlockSpec(memory_space=pltpu.VMEM)
    sems = [pltpu.SemaphoreType.DMA((n - 1,)) for n in lanes for _ in range(2)]
    return pl.pallas_call(
        functools.partial(body, counts),
        out_shape=outs,
        in_specs=[vmem] * len(operands),
        out_specs=jax.tree.map(lambda _: vmem, outs),
        scratch_shapes=sems + [pltpu.SemaphoreType.DMA((3,))],
        compiler_params=pltpu.CompilerParams(collective_id=number, has_side_effects=True),
        name=name,
    )(*operands)


def product_kernel(tile, rows, cols, wsame, wswap, out, same, swap, right):
    @pl.when((pl.program_id(0) == 0) & (pl.program_id(1) == 0))
    def _():
        groups, part, width = rows.shape
        group = rows[...].astype(f32)
        same[...] = group.reshape(groups * part, width).T
        half = part // 2
        turned = jnp.concatenate([group[:, half:], group[:, :half]], axis=1)
        swap[...] = turned.reshape(groups * part, width).T
        wide = cols.shape[3]
        for j in range(cols.shape[0]):
            block = cols[j].astype(f32).reshape(groups * part, wide)
            right[:, pl.ds(j * wide, wide)] = block.astype(bf16)

    step = pl.program_id(1)
    here = pl.ds(pl.multiple_of(step * tile, tile), tile)
    weight_same = wsame[pl.ds(pl.program_id(0), 1), :]
    weight_swap = wswap[pl.ds(pl.program_id(0), 1), :]
    other = right[...]
    out[0, 0] = dot((same[here, :] * weight_same).astype(bf16), other, ((1,), (0,)))
    out[0, 1] = dot((swap[here, :] * weight_swap).astype(bf16), other, ((1,), (0,)))


def make_product(rows, cols, wsame, wswap):
    groups, part, height = rows.shape
    depth = groups * part
    width = cols.shape[0] * cols.shape[3]
    freqs = wsame.shape[0]
    tile = 128 if height % 128 == 0 else height
    vmem = pl.BlockSpec(memory_space=pltpu.VMEM)
    return pl.pallas_call(
        functools.partial(product_kernel, tile),
        out_shape=jax.ShapeDtypeStruct((freqs, 2, height, width), f32),
        grid=(freqs, height // tile),
        in_specs=[vmem] * 4,
        out_specs=pl.BlockSpec((1, 2, tile, width), lambda w, t: (w, 0, t, 0)),
        scratch_shapes=[pltpu.VMEM((height, depth), f32)] * 2
        + [pltpu.VMEM((depth, width), bf16)],
        cost_estimate=pl.CostEstimate(
            flops=4 * freqs * depth * height * width,
            bytes_accessed=8 * freqs * height * width,
            transcendentals=0,
        ),
        name="product",
    )(rows, cols, wsame, wswap)


def per_device(
    val_wave, cond_wave, val_energy, cond_energy, frequency, kpoint_map, umklapp, gvector_index
):
    slab_count = lax.axis_size("slab")
    kpoint_count = lax.axis_size("ka")
    kpoint_here = lax.axis_index("ka")
    slab_here = lax.axis_index("slab")
    grid_side = max((candidate for candidate in range(1, 9) if candidate**3 <= kpoint_count))
    bands_v, planes, extent_y, extent_z = val_wave.shape[2:]
    bands_c = cond_wave.shape[2]
    extent_x = planes * slab_count
    local_c = bands_c // slab_count
    total_g = gvector_index.shape[0]
    points = extent_x * extent_y

    index = jnp.arange(kpoint_count, dtype=jnp.int32)
    shift_vec = jnp.sum(jnp.where(index[None, :] == kpoint_here, umklapp, 0), axis=1)
    xpos = slab_here * planes + jnp.arange(planes, dtype=jnp.int32)
    ypos = jnp.arange(extent_y, dtype=jnp.int32)
    zpos = jnp.arange(extent_z, dtype=jnp.int32)
    first_part = (shift_vec[0] * xpos % extent_x).astype(f32)[:, None, None] / extent_x
    second_part = (shift_vec[1] * ypos % extent_y).astype(f32)[None, :, None] / extent_y
    third_part = (shift_vec[2] * zpos % extent_z).astype(f32)[None, None, :] / extent_z
    angle = two_pi * (first_part + second_part + third_part)
    cosine = jnp.cos(angle)
    sine = jnp.sin(angle)
    val_re, val_im = val_wave[0, 0], val_wave[1, 0]
    turned = jnp.stack([val_re * cosine + val_im * sine, val_im * cosine - val_re * sine])
    local = planes * extent_y
    val_out = turned.reshape(2, bands_v, local, extent_z)
    cond_out = cond_wave[:, 0]
    cond_out = jnp.swapaxes(
        cond_out.reshape(2, slab_count, local_c, local, extent_z), 0, 1
    )
    level = jnp.concatenate([val_energy, cond_energy], axis=1)
    level = jnp.pad(level, ((0, 7), (0, 128 - level.shape[1])))
    counts = (kpoint_count, slab_count)
    shape_of = jax.ShapeDtypeStruct
    val_all, cond, level_all = exchange(
        spread_kernel, "spread", 0, counts, (val_out, cond_out, level),
        (
            shape_of((kpoint_count, *val_out.shape), val_out.dtype),
            shape_of(cond_out.shape, cond_out.dtype),
            shape_of((kpoint_count, *level.shape), level.dtype),
        ),
        (kpoint_count, slab_count, kpoint_count),
    )
    came = kpoint_map[None, :] == index[:, None]
    source = jnp.sum(jnp.where(kpoint_map == kpoint_here, index, 0))
    val_here = lax.dynamic_index_in_dim(val_all, source, 0, keepdims=False)
    val = exchange(
        gather_kernel, "gather", 1, counts, (val_here,),
        shape_of((slab_count, *val_here.shape), val_here.dtype), (slab_count,),
    )

    tables = (z_table(extent_z), *plane_table(extent_x, extent_y))
    norm = 1.0 / (2.0 * math.sqrt(points * extent_z))
    column_g = total_g // slab_count
    row_g = total_g // kpoint_count
    tile = row_g if row_g % 128 == 0 and column_g % row_g == 0 else column_g
    tiles = make_pairs(
        val,
        cond,
        (gvector_index // extent_z)[None],
        (gvector_index % extent_z)[None],
        tile,
        norm,
        tables,
    )
    part = tiles.shape[1]
    blocks = tiles
    if tile != row_g:
        blocks = jnp.swapaxes(tiles, 0, 1).reshape(part, kpoint_count, row_g)
        blocks = jnp.swapaxes(blocks, 0, 1)
    columns, rows = exchange(
        share_kernel, "share", 2, counts, (tiles, blocks),
        (
            shape_of((column_g // tile, slab_count, kpoint_count, part, tile), bf16),
            shape_of((slab_count, kpoint_count, part, row_g), bf16),
        ),
        (kpoint_count, slab_count, slab_count, kpoint_count),
    )
    groups = slab_count * kpoint_count
    depth = groups * part

    energies = level_all[:, 0]
    val_level = jnp.sum(
        jnp.where(came[:, :, None], energies[None, :, :bands_v], 0.0), axis=1
    )
    cond_level = energies[:, bands_v : bands_v + bands_c]
    cond_level = jnp.swapaxes(cond_level.reshape(kpoint_count, slab_count, local_c), 0, 1)
    gap = val_level[None, :, :, None] - cond_level[:, :, None, :]
    gap = gap.reshape(groups, bands_v * local_c)
    freq = frequency[:, None, None]
    weight = 2.0 * gap[None] / (gap[None] ** 2 + freq**2) / kpoint_count
    wsame = jnp.concatenate([weight, weight], axis=2).reshape(-1, depth)
    wswap = jnp.concatenate([weight, -weight], axis=2).reshape(-1, depth)
    return make_product(
        rows.reshape(groups, part, row_g),
        columns.reshape(-1, groups, part, tile),
        wsame,
        wswap,
    )


def solution(mesh):
    return jax.shard_map(
        per_device,
        mesh=mesh,
        in_specs=(
            P(None, "ka", None, "slab", None, None),
            P(None, "ka", None, "slab", None, None),
            P("ka", None),
            P("ka", None),
            P(),
            P(),
            P(),
            P(),
        ),
        out_specs=P(None, None, "ka", "slab"),
        check_vma=False,
    )
```

time: 122 us -> 98.4 us (0.81)
  blocking collectives: 50.9 us -> 0 us
  Pallas kernels: 29.5 us -> 78.4 us
  starting transfers between devices: 17 us -> 0 us
  waiting for transfers between devices: 7.99 us -> 0 us
  local copies, waits for them, and re-layouts: 5.55 us -> 7.59 us
  other arithmetic: 7.63 us -> 9.25 us
    all_gather x4 -> x0, blocking collectives: 50.9 us -> none  [the longest x1 15.9 us: per_device(): val = lax.all_gather(routed, 'slab', axis=2, tiled=True)]
    pallas_call x1 -> x4, Pallas kernels: 9.24 us -> 58.1 us  [the longest x3 49.4 us: exchange(): pl.pallas_call(functools.partial(body, counts), out_shape=outs, in_specs=...]
    all_to_all x3 -> x0, starting transfers between devices: 13.3 us -> none  [the longest x1 5.08 us: per_device(): lax.all_to_all(pair_low, 'slab', split_axis=1, concat_axis=0, tiled=True)]
    ppermute x3 -> x0, waiting for transfers between devices: 4.75 us -> none  [route(): moved = lax.ppermute(payload, 'ka', perm)]
    ppermute x3 -> x0, starting transfers between devices: 3.73 us -> none  [route(): moved = lax.ppermute(payload, 'ka', perm)]
    all_to_all x3 -> x0, waiting for transfers between devices: 3.24 us -> none  [the longest x1 3.24 us: per_device(): lax.all_to_all(pair_low.reshape(part, kpoint_count, total_g // kpoint_cou...]
    unnamed x1 -> x0, local copies, waits for them, and re-layouts: 1.78 us -> none
    another operation x0 -> x1, local copies, waits for them, and re-layouts: none -> 1.77 us  [per_device(): cond_out.reshape(2, slab_count, local_c, local, extent_z)]
  transfers between devices with their start and end apart: 6 -> 0, of which waited for: 3 -> 0; matrix products, arithmetic and copies ran while one was open for 7% -> 0% of each run, Pallas kernels for 0% -> 0%
where the time goes in v2:
time: 98.4 us; the launch traced here: 97.3 us
  Pallas kernels  78.4 us (80%)
  other arithmetic  9.25 us (9%)
  local copies, waits for them, and re-layouts  7.59 us (8%)
  between operations  2.01 us (2%)
    pallas_call x3, Pallas kernels, exchange(): pl.pallas_call(functools.partial(body, counts), out_shape=outs, in_specs=...  49.4 us
    pallas_call x1, Pallas kernels, make_product(): pl.pallas_call(functools.partial(product_kernel, tile), out_shape=jax.Sha...  20.3 us
    pallas_call x1, Pallas kernels, make_pairs(): pl.pallas_call(functools.partial(pair_kernel, norm), out_shape=jax.ShapeD...  8.69 us

profile of v2, /device:TPU:0, one launch (start us, length us, event | category | flops | bytes accessed | tf_op | source)
XLA Modules:
  0.0 97.3 jit_solution(1894494252635992697)
XLA Ops:
  0.0 1.3 %fusion.10 = s32[]{:T(128)} fusion(s32[8]{0:T(128)} %param.16, s32[]{:T(128)S(6)} %axis_index.23), kind=kLoop, calls=%fused_computation.42 | loop fusion | flops 23 | bytes 40 | tf_op jit(solution)/shard_map/reduce_sum | solution.py:328
  3.3 0.8 select_reduce_fusion.1
  4.1 0.7 integer_pow.17
  4.8 0.7 iota_compare_fusion.2
  5.4 0.6 fusion.15
  6.1 0.7 fusion.5
  6.8 0.6 fusion.9
  7.4 0.6 fusion.7
  8.1 0.1 broadcast_add_fusion
  8.1 0.1 add.126
  8.2 1.3 %select_maximum_fusion.level = f32[8,128]{1,0:T(8,128)} fusion(f32[1,8]{1,0:T(1,128)} %param.14, f32[1,2]{1,0:T(1,128)} %param.13), kind=kLoop, calls=%fused_computation.22 | loop fusion | flops 8192 | bytes 4136 | tf_op jit(solution)/shard_map/concatenate | solution.py:314
  9.6 0.2 fusion.1
  9.7 1.4 %add_select_fusion = (s32[6144]{0:T(1024)}, s32[6144]{0:T(1024)}) fusion(s32[6144]{0:T(1024)} %param.18), kind=kLoop, calls=%fused_computation.5 | loop fusion | flops 116736 | bytes 73728 | tf_op jit(solution)/shard_map/jit(remainder)/select_n | solution.py:344
  11.1 0.8 fusion.14
  11.9 0.6 pad_maximum_fusion.val
  12.6 1.8 %copy.33 = f32[2,4,2,48,128]{4,3,2,0,1:T(8,128)} copy(f32[2,4,2,48,128]{4,3,2,1,0:T(8,128)} %bitcast.27) | data formatting | bytes 786432 | tf_op jit(solution)/shard_map/reshape;squeeze | solution.py:312
  14.4 19.0 %spread.1 = (f32[8,2,2,48,128]{4,3,2,1,0:T(8,128)}, f32[4,2,2,48,128]{4,3,2,1,0:T(8,128)}, f32[8,8,128]{2,1,0:T(8,128)}) custom-call(f32[2,2,48,128]{3,2,1,0:T(8,128)} %pad_maximum_fusion.val, f32[4,2,2,48,128]{4,3,2,1,0:T(8,128)} %bitcast.24, f32[8,128]{1,0:T(8,128)} %select_maximum_fusion.level), custom_call_target="tpu_custom_call" | custom-call | tf_op jit(solution)/shard_map/spread/pallas_call | solution.py:222
  33.4 1.5 %dynamic-slice_bitcast_fusion.val = f32[2,2,48,128]{3,2,1,0:T(8,128)} fusion(f32[8,2,2,48,128]{4,3,2,1,0:T(8,128)} %get-tuple-element.10, s32[]{:T(128)S(6)} %select_n.63), kind=kLoop, calls=%fused_computation.2 | loop fusion | bytes 196612 | tf_op jit(solution)/shard_map/jit(dynamic_index_in_dim)/squeeze | solution.py:329
  34.9 0.8 slice.29
  35.7 0.1 copy.27
  35.8 0.1 select_reduce_fusion
  35.8 0.1 slice.31
  35.9 0.1 copy.28
  36.0 0.1 mul.137
  36.1 0.1 integer_pow.16
  36.2 0.1 fusion.13
  36.3 0.1 copy.31
  36.4 0.7 reshape.228.wswap
  37.1 0.1 copy.30
  37.1 0.7 reshape.227.wsame
  37.8 12.5 %gather.1.val = f32[4,2,2,48,128]{4,3,2,1,0:T(8,128)} custom-call(f32[2,2,48,128]{3,2,1,0:T(8,128)} %dynamic-slice_bitcast_fusion.val), custom_call_target="tpu_custom_call" | custom-call | tf_op jit(solution)/shard_map/gather/pallas_call | solution.py:222
  50.4 8.7 %pairs.1.tiles.blocks = bf16[8,8,768]{2,1,0:T(8,128)(2,1)} custom-call(f32[4,2,2,48,128]{4,3,2,1,0:T(8,128)} %gather.1.val, f32[4,2,2,48,128]{4,3,2,1,0:T(8,128)} %get-tuple-element.11.cond, bf16[2,256,256]{2,1,0:T(8,128)(2,1)} %constant.103.clone.ztab, bf16[2,192,192]{2,1,0:T(8,128)(2,1)} %constant.104.clone.ctab, ...), custom_call_target="tpu_custom_call" | custom-call | flops 2415919104 | bytes 2097152 | tf_op jit(solution)/shard_map/pairs/pallas_call | solution.py:106
  59.1 17.8 %share.1 = (bf16[2,4,8,8,768]{4,3,2,1,0:T(8,128)(2,1)}, bf16[4,8,8,768]{3,2,1,0:T(8,128)(2,1)}) custom-call(bf16[8,8,768]{2,1,0:T(8,128)(2,1)} %pairs.1.tiles.blocks, bf16[8,8,768]{2,1,0:T(8,128)(2,1)} %pairs.1.tiles.blocks), custom_call_target="tpu_custom_call" | custom-call | tf_op jit(solution)/shard_map/share/pallas_call | solution.py:222
  76.9 20.3 %product.1 = f32[4,2,768,1536]{3,2,1,0:T(8,128)} custom-call(bf16[32,8,768]{2,1,0:T(8,128)(2,1)} %bitcast.26, bf16[2,32,8,768]{3,2,1,0:T(8,128)(2,1)} %bitcast.25, f32[4,256]{1,0:T(4,128)} %reshape.227.wsame, f32[4,256]{1,0:T(4,128)} %reshape.228.wswap), custom_call_target="tpu_custom_call" | custom-call | flops 4831838208 | bytes 37748736 | tf_op jit(solution)/shard_map/product/pallas_call | solution.py:263
  (5 shorter events, 0.1 us)

commit v3 on v2

--- a/solution.py
+++ b/solution.py
@@ -51,7 +51,15 @@
     return dot(a[0], b[0], dims) + dot(a[1], b[0], dims) + dot(a[0], b[1], dims)
 
 
-def pair_kernel(norm, val, cond, ztab, ctab, stab, gxy, gz, out, spectrum):
+def origin(kmap):
+    here = lax.axis_index("ka")
+    source = jnp.int32(0)
+    for k in range(kmap.shape[0]):
+        source = jnp.where(kmap[k] == here, k, source)
+    return source
+
+
+def pair_kernel(norm, extent_y, kmap, fold, val, cond, ztab, ctab, stab, gvec, out, spectrum):
     blocks, _, bands_v, _, length = val.shape
     bands_c = cond.shape[2]
     pairs = bands_v * bands_c
@@ -79,12 +87,25 @@
             spectrum[pl.ds(p * length, length), :] = real.astype(bf16)
             spectrum[pl.ds((pairs + p) * length, length), :] = imag.astype(bf16)
 
+    source = origin(kmap)
+    extent_x = points // extent_y
+
+    def moved(position, direction, extent):
+        there = position - fold[direction, source]
+        return jnp.where(there < 0, there + extent, there)
+
     @pl.loop(0, out.shape[0])
     def _(step):
         cols = pl.ds(pl.multiple_of(step * tile, tile), tile)
-        chosen = lax.broadcasted_iota(jnp.int32, (points, tile), 0) == gxy[:, cols]
+        index = gvec[:, cols]
+        plane = lax.div(index, length)
+        line_x = moved(lax.div(plane, extent_y), 0, extent_x)
+        line_y = moved(lax.rem(plane, extent_y), 1, extent_y)
+        gxy = line_x * extent_y + line_y
+        gz = moved(lax.rem(index, length), 2, length)
+        chosen = lax.broadcasted_iota(jnp.int32, (points, tile), 0) == gxy
         picked = dot(spectrum[...], chosen.astype(f32).astype(bf16), ((1,), (0,)))
-        here = lax.broadcasted_iota(jnp.int32, (length, tile), 0) == gz[:, cols]
+        here = lax.broadcasted_iota(jnp.int32, (length, tile), 0) == gz
         rows = [
             jnp.sum(
                 jnp.where(here, picked[r * length : (r + 1) * length], 0.0),
@@ -96,24 +117,25 @@
         out[step] = jnp.concatenate(rows, axis=0).astype(bf16)
 
 
-def make_pairs(val, cond, gxy, gz, tile, norm, tables):
+def make_pairs(kmap, fold, val, cond, gvec, extent_y, tile, norm, tables):
     blocks, _, bands_v, rows, length = val.shape
     bands_c = cond.shape[2]
     points = blocks * rows
-    total = gxy.shape[1]
+    total = gvec.shape[1]
     part = 2 * bands_v * bands_c
     vmem = pl.BlockSpec(memory_space=pltpu.VMEM)
+    smem = pl.BlockSpec(memory_space=pltpu.SMEM)
     return pl.pallas_call(
-        functools.partial(pair_kernel, norm),
+        functools.partial(pair_kernel, norm, extent_y),
         out_shape=jax.ShapeDtypeStruct((total // tile, part, tile), bf16),
-        in_specs=[vmem] * 7,
+        in_specs=[smem] * 2 + [vmem] * 6,
         out_specs=vmem,
         scratch_shapes=[pltpu.VMEM((part * length, points), bf16)],
         cost_estimate=pl.CostEstimate(
             flops=2 * part * length * points * total, bytes_accessed=1 << 21, transcendentals=0
         ),
         name="pairs",
-    )(val, cond, *tables, gxy, gz)
+    )(kmap, fold, val, cond, *tables, gvec)
 
 
 def meet(peers):
@@ -149,31 +171,37 @@
     return copy
 
 
-def spread_kernel(counts, val, cond, level, val_all, cond_all, level_all, sa, ra, sb, rb, sc, rc, own):
+def spread_kernel(
+    counts, kmap, val, cond, level, val_all, cond_all, level_all,
+    sa, ra, sb, rb, sc, rc, sd, rd, own, bank, staged,
+):
     k, s, along_ka, along_slab = others(*counts)
+    local_c = cond_all.shape[2]
     meet(along_ka + along_slab)
-    copies = []
-    for i, peer in enumerate(along_ka):
-        copies.append(send(val, val_all.at[k], (sa, ra), i, peer))
-    for i, peer in enumerate(along_slab):
-        copies.append(send(cond.at[peer[1]], cond_all.at[s], (sb, rb), i, peer))
-    for i, peer in enumerate(along_ka):
-        copies.append(send(level, level_all.at[k], (sc, rc), i, peer))
-    copies.append(keep(val, val_all.at[k], own.at[0]))
-    copies.append(keep(cond.at[s], cond_all.at[s], own.at[1]))
-    copies.append(keep(level, level_all.at[k], own.at[2]))
-    for copy in copies:
+    to_ka = [send(val, bank.at[k], (sa, ra), i, peer) for i, peer in enumerate(along_ka)]
+    rest = [
+        send(cond.at[:, pl.ds(peer[1] * local_c, local_c)], cond_all.at[s], (sb, rb), i, peer)
+        for i, peer in enumerate(along_slab)
+    ]
+    rest += [send(level, level_all.at[k], (sc, rc), i, peer) for i, peer in enumerate(along_ka)]
+    keeps = [
+        keep(val, bank.at[k], own.at[0]),
+        keep(cond.at[:, pl.ds(s * local_c, local_c)], cond_all.at[s], own.at[1]),
+        keep(level, level_all.at[k], own.at[2]),
+    ]
+    for copy in keeps:
         copy.wait()
-
-
-def gather_kernel(counts, val, val_all, sa, ra, own):
-    k, s, _, along_slab = others(*counts)
-    meet(along_slab)
-    copies = [
-        send(val, val_all.at[s], (sa, ra), i, peer) for i, peer in enumerate(along_slab)
-    ]
-    copies.append(keep(val, val_all.at[s], own.at[0]))
-    for copy in copies:
+    for copy in to_ka:
+        copy.wait_recv()
+    chosen = bank[origin(kmap)]
+    staged[...] = chosen
+    val_all[s] = chosen
+    for copy in to_ka:
+        copy.wait_send()
+    to_slab = [
+        send(staged, val_all.at[s], (sd, rd), i, peer) for i, peer in enumerate(along_slab)
+    ]
+    for copy in rest + to_slab:
         copy.wait()
 
 
@@ -216,15 +244,16 @@
         copy.wait()
 
 
-def exchange(body, name, number, counts, operands, outs, lanes):
+def exchange(body, name, number, counts, operands, outs, lanes, scratch=(), scalars=0):
     vmem = pl.BlockSpec(memory_space=pltpu.VMEM)
+    smem = pl.BlockSpec(memory_space=pltpu.SMEM)
     sems = [pltpu.SemaphoreType.DMA((n - 1,)) for n in lanes for _ in range(2)]
     return pl.pallas_call(
         functools.partial(body, counts),
         out_shape=outs,
-        in_specs=[vmem] * len(operands),
+        in_specs=[smem] * scalars + [vmem] * (len(operands) - scalars),
         out_specs=jax.tree.map(lambda _: vmem, outs),
-        scratch_shapes=sems + [pltpu.SemaphoreType.DMA((3,))],
+        scratch_shapes=sems + [pltpu.SemaphoreType.DMA((3,)), *scratch],
         compiler_params=pltpu.CompilerParams(collective_id=number, has_side_effects=True),
         name=name,
     )(*operands)
@@ -282,9 +311,6 @@
 ):
     slab_count = lax.axis_size("slab")
     kpoint_count = lax.axis_size("ka")
-    kpoint_here = lax.axis_index("ka")
-    slab_here = lax.axis_index("slab")
-    grid_side = max((candidate for candidate in range(1, 9) if candidate**3 <= kpoint_count))
     bands_v, planes, extent_y, extent_z = val_wave.shape[2:]
     bands_c = cond_wave.shape[2]
     extent_x = planes * slab_count
@@ -293,44 +319,28 @@
     points = extent_x * extent_y
 
     index = jnp.arange(kpoint_count, dtype=jnp.int32)
-    shift_vec = jnp.sum(jnp.where(index[None, :] == kpoint_here, umklapp, 0), axis=1)
-    xpos = slab_here * planes + jnp.arange(planes, dtype=jnp.int32)
-    ypos = jnp.arange(extent_y, dtype=jnp.int32)
-    zpos = jnp.arange(extent_z, dtype=jnp.int32)
-    first_part = (shift_vec[0] * xpos % extent_x).astype(f32)[:, None, None] / extent_x
-    second_part = (shift_vec[1] * ypos % extent_y).astype(f32)[None, :, None] / extent_y
-    third_part = (shift_vec[2] * zpos % extent_z).astype(f32)[None, None, :] / extent_z
-    angle = two_pi * (first_part + second_part + third_part)
-    cosine = jnp.cos(angle)
-    sine = jnp.sin(angle)
-    val_re, val_im = val_wave[0, 0], val_wave[1, 0]
-    turned = jnp.stack([val_re * cosine + val_im * sine, val_im * cosine - val_re * sine])
     local = planes * extent_y
-    val_out = turned.reshape(2, bands_v, local, extent_z)
-    cond_out = cond_wave[:, 0]
-    cond_out = jnp.swapaxes(
-        cond_out.reshape(2, slab_count, local_c, local, extent_z), 0, 1
-    )
+    val_out = val_wave.reshape(2, bands_v, local, extent_z)
+    cond_out = cond_wave.reshape(2, bands_c, local, extent_z)
     level = jnp.concatenate([val_energy, cond_energy], axis=1)
     level = jnp.pad(level, ((0, 7), (0, 128 - level.shape[1])))
     counts = (kpoint_count, slab_count)
     shape_of = jax.ShapeDtypeStruct
-    val_all, cond, level_all = exchange(
-        spread_kernel, "spread", 0, counts, (val_out, cond_out, level),
+    val, cond, level_all = exchange(
+        spread_kernel, "spread", 0, counts, (kpoint_map, val_out, cond_out, level),
         (
-            shape_of((kpoint_count, *val_out.shape), val_out.dtype),
-            shape_of(cond_out.shape, cond_out.dtype),
-            shape_of((kpoint_count, *level.shape), level.dtype),
-        ),
-        (kpoint_count, slab_count, kpoint_count),
+            shape_of((slab_count, *val_out.shape), f32),
+            shape_of((slab_count, 2, local_c, local, extent_z), f32),
+            shape_of((kpoint_count, *level.shape), f32),
+        ),
+        (kpoint_count, slab_count, kpoint_count, slab_count),
+        (
+            pltpu.VMEM((kpoint_count, *val_out.shape), f32),
+            pltpu.VMEM(val_out.shape, f32),
+        ),
+        1,
     )
     came = kpoint_map[None, :] == index[:, None]
-    source = jnp.sum(jnp.where(kpoint_map == kpoint_here, index, 0))
-    val_here = lax.dynamic_index_in_dim(val_all, source, 0, keepdims=False)
-    val = exchange(
-        gather_kernel, "gather", 1, counts, (val_here,),
-        shape_of((slab_count, *val_here.shape), val_here.dtype), (slab_count,),
-    )
 
     tables = (z_table(extent_z), *plane_table(extent_x, extent_y))
     norm = 1.0 / (2.0 * math.sqrt(points * extent_z))
@@ -338,10 +348,12 @@
     row_g = total_g // kpoint_count
     tile = row_g if row_g % 128 == 0 and column_g % row_g == 0 else column_g
     tiles = make_pairs(
+        kpoint_map,
+        umklapp,
         val,
         cond,
-        (gvector_index // extent_z)[None],
-        (gvector_index % extent_z)[None],
+        gvector_index[None],
+        extent_y,
         tile,
         norm,
         tables,
@@ -352,7 +364,7 @@
         blocks = jnp.swapaxes(tiles, 0, 1).reshape(part, kpoint_count, row_g)
         blocks = jnp.swapaxes(blocks, 0, 1)
     columns, rows = exchange(
-        share_kernel, "share", 2, counts, (tiles, blocks),
+        share_kernel, "share", 1, counts, (tiles, blocks),
         (
             shape_of((column_g // tile, slab_count, kpoint_count, part, tile), bf16),
             shape_of((slab_count, kpoint_count, part, row_g), bf16),

time: 98.4 us -> 80.5 us (0.82)
  other arithmetic: 9.25 us -> 2.93 us
  local copies, waits for them, and re-layouts: 7.59 us -> 2.72 us
  Pallas kernels: 78.4 us -> 73.6 us
  between operations: 2.01 us -> 0.03 us
    pallas_call x3 -> x2, Pallas kernels: 49.4 us -> 44.5 us  [exchange(): pl.pallas_call(functools.partial(body, counts), out_shape=outs, in_specs=...]
    reduce_sum x2 -> x0, other arithmetic: 2.09 us -> none  [the longest x1 1.29 us: per_device(): source = jnp.sum(jnp.where(kpoint_map == kpoint_here, index, 0))]
    div x3 -> x0, other arithmetic: 1.95 us -> none  [the longest x1 0.66 us: per_device(): (shift_vec[0] * xpos % extent_x).astype(f32)[:, None, None] / extent_x]
    another operation x1 -> x0, local copies, waits for them, and re-layouts: 1.77 us -> none  [per_device(): cond_out.reshape(2, slab_count, local_c, local, extent_z)]
    squeeze x1 -> x0, local copies, waits for them, and re-layouts: 1.55 us -> none  [per_device(): val_here = lax.dynamic_index_in_dim(val_all, source, 0, keepdims=False)]
    slice x2 -> x0, local copies, waits for them, and re-layouts: 1.48 us -> none  [the longest x1 0.83 us: per_device(): val_re, val_im = (val_wave[0, 0], val_wave[1, 0])]
    select_n x1 -> x0, other arithmetic: 1.37 us -> none  [per_device(): gvector_index % extent_z]
where the time goes in v3:
time: 80.5 us; the launch traced here: 79.2 us
  Pallas kernels  73.6 us (91%)
  other arithmetic  2.93 us (4%)
  local copies, waits for them, and re-layouts  2.72 us (3%)
    pallas_call x2, Pallas kernels, exchange(): pl.pallas_call(functools.partial(body, counts), out_shape=outs, in_specs=...  44.5 us
    pallas_call x1, Pallas kernels, make_product(): pl.pallas_call(functools.partial(product_kernel, tile), out_shape=jax.Sha...  20.3 us
    pallas_call x1, Pallas kernels, make_pairs(): pl.pallas_call(functools.partial(pair_kernel, norm, extent_y), out_shape=...  8.81 us

profile of v3, /device:TPU:0, one launch (start us, length us, event | category | flops | bytes accessed | tf_op | source)
XLA Modules:
  0.0 79.2 jit_solution(7125919061027570434)
XLA Ops:
  0.0 0.7 integer_pow.17
  0.7 0.7 iota_compare_fusion.2
  1.4 1.3 %select_maximum_fusion.level = f32[8,128]{1,0:T(8,128)} fusion(f32[1,8]{1,0:T(1,128)} %param.14, f32[1,2]{1,0:T(1,128)} %param.13), kind=kLoop, calls=%fused_computation.6 | loop fusion | flops 8192 | bytes 4136 | tf_op jit(solution)/shard_map/concatenate | solution.py:325
  2.7 25.4 %spread.1 = (f32[4,2,2,48,128]{4,3,2,1,0:T(8,128)}, f32[4,2,2,48,128]{4,3,2,1,0:T(8,128)}, f32[8,8,128]{2,1,0:T(8,128)}) custom-call(s32[8]{0:T(128)} %kmap.3, f32[2,2,48,128]{3,2,1,0:T(8,128)} %bitcast.17, f32[2,8,48,128]{3,2,1,0:T(8,128)} %bitcast.16, f32[8,128]{1,0:T(8,128)} %select_maximum_fusion.level), custom_call_target="tpu_custom_call" | custom-call | tf_op jit(solution)/shard_map/spread/pallas_call | solution.py:251
  28.1 8.8 %pairs.1.tiles.blocks = bf16[8,8,768]{2,1,0:T(8,128)(2,1)} custom-call(s32[8]{0:T(128)} %kmap.3, s32[3,8]{1,0:T(4,128)} %fold.1, f32[4,2,2,48,128]{4,3,2,1,0:T(8,128)} %get-tuple-element.10.val, f32[4,2,2,48,128]{4,3,2,1,0:T(8,128)} %get-tuple-element.11.cond, bf16[2,256,256]{2,1,0:T(8,128)(2,1)} %constant.15.clone.ztab, ...), custom_call_target="tpu_custom_call" | custom-call | flops 2415919104 | bytes 2097152 | tf_op jit(solution)/shard_map/pairs/pallas_call | solution.py:128
  36.9 0.8 slice.9
  37.7 0.1 copy.24
  37.8 0.1 select_reduce_fusion
  37.8 0.1 slice.11
  37.9 0.1 copy.25
  38.0 0.1 mul.16
  38.1 0.1 integer_pow.16
  38.2 0.1 fusion
  38.3 0.1 copy.28
  38.4 0.7 reshape.79.wswap
  39.1 0.1 copy.27
  39.1 0.7 reshape.78.wsame
  39.8 19.1 %share.1 = (bf16[2,4,8,8,768]{4,3,2,1,0:T(8,128)(2,1)}, bf16[4,8,8,768]{3,2,1,0:T(8,128)(2,1)}) custom-call(bf16[8,8,768]{2,1,0:T(8,128)(2,1)} %pairs.1.tiles.blocks, bf16[8,8,768]{2,1,0:T(8,128)(2,1)} %pairs.1.tiles.blocks), custom_call_target="tpu_custom_call" | custom-call | tf_op jit(solution)/shard_map/share/pallas_call | solution.py:251
  59.0 20.3 %product.1 = f32[4,2,768,1536]{3,2,1,0:T(8,128)} custom-call(bf16[32,8,768]{2,1,0:T(8,128)(2,1)} %bitcast.15, bf16[2,32,8,768]{3,2,1,0:T(8,128)(2,1)} %bitcast.14, f32[4,256]{1,0:T(4,128)} %reshape.78.wsame, f32[4,256]{1,0:T(4,128)} %reshape.79.wswap), custom_call_target="tpu_custom_call" | custom-call | flops 4831838208 | bytes 37748736 | tf_op jit(solution)/shard_map/product/pallas_call | solution.py:292
  (3 shorter events, 0.0 us)

commit v4 on v3

--- a/solution.py
+++ b/solution.py
@@ -173,12 +173,19 @@
 
 def spread_kernel(
     counts, kmap, val, cond, level, val_all, cond_all, level_all,
-    sa, ra, sb, rb, sc, rc, sd, rd, own, bank, staged,
+    sa, ra, sb, rb, sc, rc, sd, rd, se, re, own, bank, staged,
 ):
     k, s, along_ka, along_slab = others(*counts)
     local_c = cond_all.shape[2]
     meet(along_ka + along_slab)
-    to_ka = [send(val, bank.at[k], (sa, ra), i, peer) for i, peer in enumerate(along_ka)]
+    count = counts[0]
+    partner = (k + 1 - 2 * lax.rem(k, 2), s)
+    steps = range(2, count, 2)
+    to_ka = [
+        send(val, bank.at[k], (sa, ra), i, (lax.rem(k + d, count), s))
+        for i, d in enumerate(steps)
+    ]
+    to_partner = [send(val, bank.at[k], (se, re), 0, partner)]
     rest = [
         send(cond.at[:, pl.ds(peer[1] * local_c, local_c)], cond_all.at[s], (sb, rb), i, peer)
         for i, peer in enumerate(along_slab)
@@ -191,12 +198,16 @@
     ]
     for copy in keeps:
         copy.wait()
-    for copy in to_ka:
+    for i, d in enumerate(steps):
+        to_ka[i].wait_recv()
+        block = bank.at[lax.rem(k + count - d, count)]
+        to_partner.append(send(block, block, (se, re), i + 1, partner))
+    for copy in to_partner:
         copy.wait_recv()
     chosen = bank[origin(kmap)]
     staged[...] = chosen
     val_all[s] = chosen
-    for copy in to_ka:
+    for copy in to_ka + to_partner:
         copy.wait_send()
     to_slab = [
         send(staged, val_all.at[s], (sd, rd), i, peer) for i, peer in enumerate(along_slab)
@@ -333,7 +344,7 @@
             shape_of((slab_count, 2, local_c, local, extent_z), f32),
             shape_of((kpoint_count, *level.shape), f32),
         ),
-        (kpoint_count, slab_count, kpoint_count, slab_count),
+        (kpoint_count // 2, slab_count, kpoint_count, slab_count, kpoint_count // 2 + 1),
         (
             pltpu.VMEM((kpoint_count, *val_out.shape), f32),
             pltpu.VMEM(val_out.shape, f32),

time: 80.5 us -> 78.9 us (0.980)
  Pallas kernels: 73.6 us -> 72.3 us
    pallas_call x2, Pallas kernels: 44.5 us -> 43.2 us  [exchange(): pl.pallas_call(functools.partial(body, counts), out_shape=outs, in_specs=...]
where the time goes in v4:
time: 78.9 us; the launch traced here: 78 us
  Pallas kernels  72.3 us (92%)
  other arithmetic  2.93 us (4%)
  local copies, waits for them, and re-layouts  2.72 us (3%)
    pallas_call x2, Pallas kernels, exchange(): pl.pallas_call(functools.partial(body, counts), out_shape=outs, in_specs=...  43.2 us
    pallas_call x1, Pallas kernels, make_product(): pl.pallas_call(functools.partial(product_kernel, tile), out_shape=jax.Sha...  20.3 us
    pallas_call x1, Pallas kernels, make_pairs(): pl.pallas_call(functools.partial(pair_kernel, norm, extent_y), out_shape=...  8.81 us

profile of v4, /device:TPU:0, one launch (start us, length us, event | category | flops | bytes accessed | tf_op | source)
XLA Modules:
  0.0 78.0 jit_solution(8078209642401580630)
XLA Ops:
  0.0 0.7 integer_pow.17
  0.7 0.7 iota_compare_fusion.2
  1.4 1.3 %select_maximum_fusion.level = f32[8,128]{1,0:T(8,128)} fusion(f32[1,8]{1,0:T(1,128)} %param.14, f32[1,2]{1,0:T(1,128)} %param.13), kind=kLoop, calls=%fused_computation.6 | loop fusion | flops 8192 | bytes 4136 | tf_op jit(solution)/shard_map/concatenate | solution.py:336
  2.7 25.2 %spread.1 = (f32[4,2,2,48,128]{4,3,2,1,0:T(8,128)}, f32[4,2,2,48,128]{4,3,2,1,0:T(8,128)}, f32[8,8,128]{2,1,0:T(8,128)}) custom-call(s32[8]{0:T(128)} %kmap.3, f32[2,2,48,128]{3,2,1,0:T(8,128)} %bitcast.17, f32[2,8,48,128]{3,2,1,0:T(8,128)} %bitcast.16, f32[8,128]{1,0:T(8,128)} %select_maximum_fusion.level), custom_call_target="tpu_custom_call" | custom-call | tf_op jit(solution)/shard_map/spread/pallas_call | solution.py:262
  27.9 8.8 %pairs.1.tiles.blocks = bf16[8,8,768]{2,1,0:T(8,128)(2,1)} custom-call(s32[8]{0:T(128)} %kmap.3, s32[3,8]{1,0:T(4,128)} %fold.1, f32[4,2,2,48,128]{4,3,2,1,0:T(8,128)} %get-tuple-element.10.val, f32[4,2,2,48,128]{4,3,2,1,0:T(8,128)} %get-tuple-element.11.cond, bf16[2,256,256]{2,1,0:T(8,128)(2,1)} %constant.15.clone.ztab, ...), custom_call_target="tpu_custom_call" | custom-call | flops 2415919104 | bytes 2097152 | tf_op jit(solution)/shard_map/pairs/pallas_call | solution.py:128
  36.7 0.8 slice.9
  37.5 0.1 copy.24
  37.6 0.1 select_reduce_fusion
  37.7 0.1 slice.11
  37.7 0.1 copy.25
  37.8 0.1 mul.16
  37.9 0.1 integer_pow.16
  38.0 0.1 fusion
  38.1 0.1 copy.28
  38.2 0.7 reshape.79.wswap
  38.9 0.1 copy.27
  39.0 0.7 reshape.78.wsame
  39.7 18.1 %share.1 = (bf16[2,4,8,8,768]{4,3,2,1,0:T(8,128)(2,1)}, bf16[4,8,8,768]{3,2,1,0:T(8,128)(2,1)}) custom-call(bf16[8,8,768]{2,1,0:T(8,128)(2,1)} %pairs.1.tiles.blocks, bf16[8,8,768]{2,1,0:T(8,128)(2,1)} %pairs.1.tiles.blocks), custom_call_target="tpu_custom_call" | custom-call | tf_op jit(solution)/shard_map/share/pallas_call | solution.py:262
  57.7 20.3 %product.1 = f32[4,2,768,1536]{3,2,1,0:T(8,128)} custom-call(bf16[32,8,768]{2,1,0:T(8,128)(2,1)} %bitcast.15, bf16[2,32,8,768]{3,2,1,0:T(8,128)(2,1)} %bitcast.14, f32[4,256]{1,0:T(4,128)} %reshape.78.wsame, f32[4,256]{1,0:T(4,128)} %reshape.79.wswap), custom_call_target="tpu_custom_call" | custom-call | flops 4831838208 | bytes 37748736 | tf_op jit(solution)/shard_map/product/pallas_call | solution.py:303
  (3 shorter events, 0.0 us)

commit v5 on v4

--- a/solution.py
+++ b/solution.py
@@ -216,7 +216,7 @@
         copy.wait()
 
 
-def share_kernel(counts, tiles, blocks, cols_all, rows_all, sa, ra, sb, rb, sc, rc, sd, rd, own):
+def share_kernel(counts, tiles, blocks, cols_all, rows_all, sa, ra, sb, rb, sc, rc, sd, rd, se, re, own):
     k, s, along_ka, along_slab = others(*counts)
     per_column = cols_all.shape[0]
     meet(along_ka + along_slab)
@@ -245,13 +245,23 @@
     ]
     for copy in col_first:
         copy.wait_recv()
+    count = counts[0]
+    partner = (k + 1 - 2 * lax.rem(k, 2), s)
+    steps = range(2, count, 2)
+    block = cols_all.at[:, :, k]
     col_next = [
-        send(cols_all.at[:, :, k], cols_all.at[:, :, k], (sd, rd), i, peer)
-        for i, peer in enumerate(along_ka)
-    ]
+        send(block, block, (sd, rd), i, (lax.rem(k + d, count), s)) for i, d in enumerate(steps)
+    ]
+    to_partner = [send(block, block, (se, re), 0, partner)]
+    for i, d in enumerate(steps):
+        col_next[i].wait_recv()
+        block = cols_all.at[:, :, lax.rem(k + count - d, count)]
+        to_partner.append(send(block, block, (se, re), i + 1, partner))
+    for copy in col_next:
+        copy.wait_send()
     for copy in row_first + col_first:
         copy.wait_send()
-    for copy in row_next + col_next:
+    for copy in row_next + to_partner:
         copy.wait()
 
 
@@ -270,7 +280,7 @@
     )(*operands)
 
 
-def product_kernel(tile, rows, cols, wsame, wswap, out, same, swap, right):
+def product_kernel(tile, rows, cols, wsame, out, same, swap, right):
     @pl.when((pl.program_id(0) == 0) & (pl.program_id(1) == 0))
     def _():
         groups, part, width = rows.shape
@@ -287,13 +297,15 @@
     step = pl.program_id(1)
     here = pl.ds(pl.multiple_of(step * tile, tile), tile)
     weight_same = wsame[pl.ds(pl.program_id(0), 1), :]
-    weight_swap = wswap[pl.ds(pl.program_id(0), 1), :]
+    part = rows.shape[1]
+    lane = lax.broadcasted_iota(jnp.int32, weight_same.shape, 1)
+    weight_swap = jnp.where(lax.rem(lane, part) < part // 2, weight_same, -weight_same)
     other = right[...]
     out[0, 0] = dot((same[here, :] * weight_same).astype(bf16), other, ((1,), (0,)))
     out[0, 1] = dot((swap[here, :] * weight_swap).astype(bf16), other, ((1,), (0,)))
 
 
-def make_product(rows, cols, wsame, wswap):
+def make_product(rows, cols, wsame):
     groups, part, height = rows.shape
     depth = groups * part
     width = cols.shape[0] * cols.shape[3]
@@ -304,7 +316,7 @@
         functools.partial(product_kernel, tile),
         out_shape=jax.ShapeDtypeStruct((freqs, 2, height, width), f32),
         grid=(freqs, height // tile),
-        in_specs=[vmem] * 4,
+        in_specs=[vmem] * 3,
         out_specs=pl.BlockSpec((1, 2, tile, width), lambda w, t: (w, 0, t, 0)),
         scratch_shapes=[pltpu.VMEM((height, depth), f32)] * 2
         + [pltpu.VMEM((depth, width), bf16)],
@@ -314,7 +326,7 @@
             transcendentals=0,
         ),
         name="product",
-    )(rows, cols, wsame, wswap)
+    )(rows, cols, wsame)
 
 
 def per_device(
@@ -380,7 +392,7 @@
             shape_of((column_g // tile, slab_count, kpoint_count, part, tile), bf16),
             shape_of((slab_count, kpoint_count, part, row_g), bf16),
         ),
-        (kpoint_count, slab_count, slab_count, kpoint_count),
+        (kpoint_count, slab_count, slab_count, kpoint_count // 2, kpoint_count // 2 + 1),
     )
     groups = slab_count * kpoint_count
     depth = groups * part
@@ -396,12 +408,10 @@
     freq = frequency[:, None, None]
     weight = 2.0 * gap[None] / (gap[None] ** 2 + freq**2) / kpoint_count
     wsame = jnp.concatenate([weight, weight], axis=2).reshape(-1, depth)
-    wswap = jnp.concatenate([weight, -weight], axis=2).reshape(-1, depth)
     return make_product(
         rows.reshape(groups, part, row_g),
         columns.reshape(-1, groups, part, tile),
         wsame,
-        wswap,
     )
 
 

time: 78.9 us -> 76.7 us (0.972)
  Pallas kernels: 72.3 us -> 71.5 us
    pallas_call x2, Pallas kernels: 43.2 us -> 42.4 us  [exchange(): pl.pallas_call(functools.partial(body, counts), out_shape=outs, in_specs=...]
where the time goes in v5:
time: 76.7 us; the launch traced here: 76.4 us
  Pallas kernels  71.5 us (93%)
  other arithmetic  2.92 us (4%)
  local copies, waits for them, and re-layouts  1.94 us (3%)
    pallas_call x2, Pallas kernels, exchange(): pl.pallas_call(functools.partial(body, counts), out_shape=outs, in_specs=...  42.4 us
    pallas_call x1, Pallas kernels, make_product(): pl.pallas_call(functools.partial(product_kernel, tile), out_shape=jax.Sha...  20.3 us
    pallas_call x1, Pallas kernels, make_pairs(): pl.pallas_call(functools.partial(pair_kernel, norm, extent_y), out_shape=...  8.81 us

profile of v5, /device:TPU:0, one launch (start us, length us, event | category | flops | bytes accessed | tf_op | source)
XLA Modules:
  0.0 76.4 jit_solution(10633835281650121607)
XLA Ops:
  0.0 0.7 integer_pow.17
  0.7 0.7 iota_compare_fusion.2
  1.4 1.3 %select_maximum_fusion.level = f32[8,128]{1,0:T(8,128)} fusion(f32[1,8]{1,0:T(1,128)} %param.14, f32[1,2]{1,0:T(1,128)} %param.13), kind=kLoop, calls=%fused_computation.5 | loop fusion | flops 8192 | bytes 4136 | tf_op jit(solution)/shard_map/concatenate | solution.py:348
  2.7 25.2 %spread.1 = (f32[4,2,2,48,128]{4,3,2,1,0:T(8,128)}, f32[4,2,2,48,128]{4,3,2,1,0:T(8,128)}, f32[8,8,128]{2,1,0:T(8,128)}) custom-call(s32[8]{0:T(128)} %kmap.3, f32[2,2,48,128]{3,2,1,0:T(8,128)} %bitcast.17, f32[2,8,48,128]{3,2,1,0:T(8,128)} %bitcast.16, f32[8,128]{1,0:T(8,128)} %select_maximum_fusion.level), custom_call_target="tpu_custom_call" | custom-call | tf_op jit(solution)/shard_map/spread/pallas_call | solution.py:272
  27.9 8.8 %pairs.1.tiles.blocks = bf16[8,8,768]{2,1,0:T(8,128)(2,1)} custom-call(s32[8]{0:T(128)} %kmap.3, s32[3,8]{1,0:T(4,128)} %fold.1, f32[4,2,2,48,128]{4,3,2,1,0:T(8,128)} %get-tuple-element.10.val, f32[4,2,2,48,128]{4,3,2,1,0:T(8,128)} %get-tuple-element.11.cond, bf16[2,256,256]{2,1,0:T(8,128)(2,1)} %constant.15.clone.ztab, ...), custom_call_target="tpu_custom_call" | custom-call | flops 2415919104 | bytes 2097152 | tf_op jit(solution)/shard_map/pairs/pallas_call | solution.py:128
  36.7 0.8 slice.9
  37.5 0.1 copy.23
  37.6 0.1 select_reduce_fusion
  37.7 0.1 slice.11
  37.7 0.1 copy.24
  37.8 0.1 mul.16
  37.9 0.1 integer_pow.16
  38.0 0.1 divide_multiply_fusion
  38.1 0.1 copy.26
  38.2 0.7 reshape.75.wsame
  38.9 17.3 %share.1 = (bf16[2,4,8,8,768]{4,3,2,1,0:T(8,128)(2,1)}, bf16[4,8,8,768]{3,2,1,0:T(8,128)(2,1)}) custom-call(bf16[8,8,768]{2,1,0:T(8,128)(2,1)} %pairs.1.tiles.blocks, bf16[8,8,768]{2,1,0:T(8,128)(2,1)} %pairs.1.tiles.blocks), custom_call_target="tpu_custom_call" | custom-call | tf_op jit(solution)/shard_map/share/pallas_call | solution.py:272
  56.1 20.3 %product.1 = f32[4,2,768,1536]{3,2,1,0:T(8,128)} custom-call(bf16[32,8,768]{2,1,0:T(8,128)(2,1)} %bitcast.15, bf16[2,32,8,768]{3,2,1,0:T(8,128)(2,1)} %bitcast.14, f32[4,256]{1,0:T(4,128)} %reshape.75.wsame), custom_call_target="tpu_custom_call" | custom-call | flops 4831838208 | bytes 37748736 | tf_op jit(solution)/shard_map/product/pallas_call | solution.py:315
  (3 shorter events, 0.0 us)
